TPU v7x, 256 devices: a whole 4x4x8 slice. The times are simulated.
256 devices in a mesh: depth: 32 (over z, x_lo, core), band: 8 (over y, x_hi).
Axes of the slice: x: 4 (x_hi: 2, x_lo: 2; x = x_hi * 2 + x_lo), y: 4, z: 8, core: 2. Of those that a mesh axis runs over, the one named last changes fastest.
Arguments:
- volume: int32 [128, 256, 1024], P('depth', 'band'), may hold values from 0 to 255
- tf_table: int32 [4, 256], replicated, may hold values from 0 to 255
- view_code: int32 [2, 4], replicated, may hold values from -20 to 20
Outputs:
- final_image: float32 [2, 1024, 4, 256], P(None, 'depth', None, 'band')
All inputs are finite; a program needn't handle non-finite values.
Results may differ from a plain program's by a relative error of at most 0.0014.
Values may be sent and summed in bfloat16 or wider, within the bound.
No kernel may reach another device: no remote copies, remote signals or barrier semaphores. Data moves between devices by JAX's collectives and lax.ppermute only.
A program may use at most 64 MiB of HBM per device.

v0:
```python
import math

import jax
import jax.numpy as jnp
from jax import lax
from jax.sharding import PartitionSpec as P

VIEWS = 2
MARGIN = 16


def extended(x, sides, width):
    for axis, dim in sides:
        size, length = (lax.axis_size(axis), x.shape[dim])
        up = [(i, (i + 1) % size) for i in range(size - 1)]
        down = [(j, i) for i, j in up]
        last = lax.slice_in_dim(x, length - width, length, axis=dim)
        first = lax.slice_in_dim(x, 0, width, axis=dim)
        before = lax.ppermute(last, axis, up)
        after = lax.ppermute(first, axis, down)
        x = jnp.concatenate([before, x, after], axis=dim)
    return x


def lanczos(offset):
    return jnp.where(jnp.abs(offset) < 3.0, jnp.sinc(offset) * jnp.sinc(offset / 3.0), 0.0)


def split_offset(coefficient, position, length, lift=0):
    numerator = coefficient * (2 * position + 1 - length) + lift * length
    integer_part = numerator // (2 * length)
    fraction = (numerator - integer_part * (2 * length)).astype(jnp.float32) / (2.0 * length)
    return (integer_part, fraction)


def make_palette(tf_table, depth_count):
    table_float = tf_table.astype(jnp.float32)
    opacity = table_float[3] / (64.0 * depth_count)
    premult = table_float[0:3] / 255.0 * opacity
    return jnp.concatenate([premult, opacity[None]], axis=0).astype(jnp.bfloat16)


def classify(codes, palette):
    shape = codes.shape
    last = shape[-1]
    rows = codes.reshape(-1, last)
    row_count = rows.shape[0]
    group_rows = math.gcd(row_count, 8)
    grouped = rows.reshape(row_count // group_rows, group_rows, last)
    table = palette.reshape(4, 16, 16)
    levels = jnp.arange(16, dtype=jnp.int32)

    def lookup(block_codes):
        high_part = block_codes // 16
        low_part = block_codes - high_part * 16
        low_hot = (low_part[None] == levels[:, None, None]).astype(jnp.bfloat16)
        partial_value = jnp.einsum(
            "chl,lgk->chgk", table, low_hot, preferred_element_type=jnp.float32
        )
        high_hot = (high_part[None] == levels[:, None, None]).astype(jnp.float32)
        return jnp.sum(partial_value * high_hot[None], axis=1)

    picked = lax.map(lookup, grouped)
    picked = jnp.transpose(picked, (1, 0, 2, 3)).reshape((4,) + shape)
    return picked.astype(jnp.bfloat16)


def column_weights(integer_part, fraction, block):
    inputs = jnp.arange(3 * block, dtype=jnp.int32)[:, None]
    outputs = jnp.arange(block, dtype=jnp.int32)[None, :]
    distance = inputs - block - outputs - integer_part
    return lanczos(fraction - distance.astype(jnp.float32)).astype(jnp.bfloat16)


def row_weights(integer_part, fraction, out_rows, in_rows, margin):
    outputs = jnp.arange(out_rows, dtype=jnp.int32)[:, None]
    inputs = jnp.arange(in_rows, dtype=jnp.int32)[None, :]
    distance = inputs - margin - outputs - integer_part
    return lanczos(fraction - distance.astype(jnp.float32)).astype(jnp.bfloat16)


def warp_weights(coefficient, first_column, strip_width, margin, total_width):
    columns = first_column + jnp.arange(strip_width, dtype=jnp.int32)
    integer_part, fraction = split_offset(coefficient, columns, total_width, 1)
    inputs = jnp.arange(strip_width + 2 * margin, dtype=jnp.int32)[None, :]
    outputs = jnp.arange(strip_width, dtype=jnp.int32)[:, None]
    distance = inputs - margin - outputs - integer_part[:, None]
    return lanczos(fraction[:, None] - distance.astype(jnp.float32))


def shear_columns(source, tap_matrix, block):
    channels, row_count, extent = source.shape
    blocks = extent // block
    padded = jnp.pad(source, ((0, 0), (0, 0), (block, block)))
    tile_view = padded.reshape(channels, row_count, blocks + 2, block)
    windows = jnp.concatenate(
        [
            tile_view[:, :, 0:blocks],
            tile_view[:, :, 1 : blocks + 1],
            tile_view[:, :, 2 : blocks + 2],
        ],
        axis=3,
    )
    result = jnp.einsum("crbk,kj->bjcr", windows, tap_matrix, preferred_element_type=jnp.float32)
    return result.reshape(extent, channels, row_count).astype(jnp.bfloat16)


def shear_rows(source, tap_matrix):
    return jnp.einsum("xcr,yr->xcy", source, tap_matrix, preferred_element_type=jnp.float32)


def over(front_part, back_part):
    return front_part + (1.0 - front_part[..., 3:4, :]) * back_part


def body(volume, tf_table, view_code):
    slab_count, band_rows, extent = volume.shape
    depth_size = lax.axis_size("depth")
    depth_rank = lax.axis_index("depth")
    total_depth = slab_count * depth_size
    block = min(128, extent)
    strip_width = extent // depth_size
    widened_rows = band_rows + 2 * MARGIN
    palette = make_palette(tf_table, total_depth)
    classified = classify(volume, palette)
    finals = []
    for view_index in range(VIEWS):
        params = view_code[view_index]
        facing = params[3] >= 0
        shifted_list = []
        for slice_index in range(slab_count):
            global_slice = depth_rank * slab_count + slice_index
            whole_x, frac_x = split_offset(params[0], global_slice, total_depth)
            shifted_list.append(
                shear_columns(
                    classified[:, slice_index], column_weights(whole_x, frac_x, block), block
                )
            )
        stacked = jnp.stack(shifted_list)
        sheared_wide = extended(stacked, (("band", 3),), MARGIN)
        picture = jnp.zeros((extent, 4, band_rows), jnp.float32)
        for step_index in range(slab_count):
            local_slice = jnp.where(facing, step_index, slab_count - 1 - step_index).astype(
                jnp.int32
            )
            global_slice = depth_rank * slab_count + local_slice
            whole_y, frac_y = split_offset(params[1], global_slice, total_depth)
            row_sheared = lax.dynamic_index_in_dim(sheared_wide, local_slice, 0, keepdims=False)
            sheared = shear_rows(
                row_sheared, row_weights(whole_y, frac_y, band_rows, widened_rows, MARGIN)
            )
            picture = over(picture, sheared)
        pieces = picture.reshape(depth_size, strip_width, 4, band_rows)
        arrived = lax.all_to_all(
            pieces.astype(jnp.bfloat16), "depth", split_axis=0, concat_axis=0, tiled=True
        ).astype(pieces.dtype)
        for level_index in range(depth_size.bit_length() - 1):
            paired = arrived.reshape((arrived.shape[0] // 2, 2) + arrived.shape[1:])
            earlier = paired[:, 0]
            later = paired[:, 1]
            front_part = jnp.where(facing, earlier, later)
            back_part = jnp.where(facing, later, earlier)
            arrived = over(front_part, back_part)
        strip = arrived[0]
        padded_strip = extended(strip, (("depth", 0),), MARGIN)
        weights = warp_weights(params[2], depth_rank * strip_width, strip_width, MARGIN, extent)
        final_strip = jnp.einsum(
            "ck,kay->cay",
            weights,
            padded_strip,
            precision=lax.Precision.HIGHEST,
            preferred_element_type=jnp.float32,
        )
        finals.append(final_strip)
    return jnp.stack(finals)


def solution(mesh):
    placed = (P("depth", "band", None), P(), P())
    return jax.shard_map(
        body, mesh=mesh, in_specs=placed, out_specs=P(None, "depth", None, "band"), check_vma=False
    )
```

profile of v0, /device:TPU:9, one launch (start us, length us, event | category | flops | bytes accessed | tf_op | source)
XLA Modules:
  0.0 135.3 jit_solution(13242470006313508620)
XLA Ops:
  0.7 1.7 %fusion.1214 = (s32[1,1]{1,0:T(1,128)}, s32[1,1]{1,0:T(1,128)}, s32[1,1]{1,0:T(1,128)}, s32[1,1]{1,0:T(1,128)}, s32[1,1]{1,0:T(1,128)}, /*index=5*/s32[1,1]{1,0:T(1,128)}, s32[1,1]{1,0:T(1,128)}, s32[1,1]{1,0:T(1,128)}) fusion(s32[2,4]{1,0:T(2,128)} %param.9), kind=kLoop, calls=%fused_computation.1730 | loop fusion | bytes 64 | tf_op jit(solution)/shard_map/slice | solution.py:166
  5.0 24.4 %while.14 = (s32[]{:T(128)}, bf16[16,4,8,1024]{3,2,0,1:T(8,128)(2,1)S(1)}, s32[16,8,1024]{2,1,0:T(8,128)}, bf16[4,16,16]{2,1,0:T(8,128)(2,1)S(1)}, s32[]{:T(128)}) while((s32[]{:T(128)}, bf16[16,4,8,1024]{3,2,0,1:T(8,128)(2,1)S(1)}, s32[16,8,1024]{2,1,0:T(8,128)}, bf16[4,16,16]{2,1,0:T(8,128)(2,1)S(1)}, s32[]{:T(128)}) %tuple.70), condition=%wide.region_2.5_spmd.clone.clone, body=%wide.region_0.4_spmd.clone.clone.sunk | while | flops 18325504 | bytes 1411149 | solution.py:63
  31.0 1.0 pad.18
  33.7 0.8 fusion.23
  34.8 1.0 copy_dynamic-update-slice_fusion.9
  36.0 0.8 fusion.24
  37.4 0.8 fusion.25
  40.0 1.1 fusion.1209
  41.1 4.6 %collective-permute-start.4 = (bf16[4,1024,4,16]{1,3,2,0:T(8,128)(2,1)}, bf16[4,1024,4,16]{1,3,2,0:T(8,128)(2,1)}, u32[]{:S(2)}, u32[]{:S(2)}) collective-permute-start(bf16[4,1024,4,16]{1,3,2,0:T(8,128)(2,1)} %get-tuple-element.121), channel_id=1, source_target_pairs={{0,1},{1,2},{2,3},{3,4},{4,5},{5,6},{6,7},{8,9},{9,10},{10,11},{11... | collective-permute-start | bytes 1572872 | tf_op jit(solution)/shard_map/ppermute | solution.py:19
  45.7 3.2 %collective-permute-start.5 = (bf16[4,1024,4,16]{1,3,2,0:T(8,128)(2,1)}, bf16[4,1024,4,16]{1,3,2,0:T(8,128)(2,1)}, u32[]{:S(2)}, u32[]{:S(2)}) collective-permute-start(bf16[4,1024,4,16]{1,3,2,0:T(8,128)(2,1)} %get-tuple-element.122), channel_id=1, source_target_pairs={{1,0},{2,1},{3,2},{4,3},{5,4},{6,5},{7,6},{9,8},{10,9},{11,10},{12... | collective-permute-start | bytes 1572872 | tf_op jit(solution)/shard_map/ppermute | solution.py:20
  52.4 2.0 %fusion.20 = bf16[8,128,4,32]{1,3,0,2:T(8,128)(2,1)S(1)} fusion(bf16[4,32,8,384]{3,1,2,0:T(8,128)(2,1)} %copy-done.2, s32[]{:T(128)S(6)} %select_n.506, f32[]{:T(128)S(6)} %div.283, s32[384]{0:T(512)S(1)} %iota_add_fusion), kind=kOutput, calls=%fused_computation.44 | convolution fusion | flops 104480768 | bytes 1050120 | tf_op jit(solution)/shard_map/crbk,kj->bjcr/dot_general | solution.py:104
  54.7 0.8 fusion.21
  55.8 2.0 %fusion.22 = bf16[8,128,4,32]{1,3,0,2:T(8,128)(2,1)S(1)} fusion(bf16[4,32,8,384]{3,1,2,0:T(8,128)(2,1)} %copy-done.5, s32[]{:T(128)S(6)} %select_n.510, f32[]{:T(128)S(6)} %div.293, s32[384]{0:T(512)S(1)} %iota_add_fusion), kind=kOutput, calls=%fused_computation.46 | convolution fusion | flops 104480768 | bytes 1050120 | tf_op jit(solution)/shard_map/crbk,kj->bjcr/dot_general | solution.py:104
  58.1 1.1 fusion.1208
  59.2 3.7 %collective-permute-start = (bf16[4,1024,4,16]{1,3,2,0:T(8,128)(2,1)}, bf16[4,1024,4,16]{1,3,2,0:T(8,128)(2,1)}, u32[]{:S(2)}, u32[]{:S(2)}) collective-permute-start(bf16[4,1024,4,16]{1,3,2,0:T(8,128)(2,1)} %get-tuple-element.117), channel_id=1, source_target_pairs={{0,1},{1,2},{2,3},{3,4},{4,5},{5,6},{6,7},{8,9},{9,10},{10,11},{11... | collective-permute-start | bytes 1572872 | tf_op jit(solution)/shard_map/ppermute | solution.py:19
  62.9 4.0 %collective-permute-start.1 = (bf16[4,1024,4,16]{1,3,2,0:T(8,128)(2,1)}, bf16[4,1024,4,16]{1,3,2,0:T(8,128)(2,1)}, u32[]{:S(2)}, u32[]{:S(2)}) collective-permute-start(bf16[4,1024,4,16]{1,3,2,0:T(8,128)(2,1)} %get-tuple-element.118), channel_id=1, source_target_pairs={{1,0},{2,1},{3,2},{4,3},{5,4},{6,5},{7,6},{9,8},{10,9},{11,10},{12... | collective-permute-start | bytes 1572872 | tf_op jit(solution)/shard_map/ppermute | solution.py:20
  73.7 1.1 and_select_fusion
  74.9 1.1 convert_multiply_fusion
  76.0 1.4 %pad_maximum_fusion.1 = bf16[4,1024,4,64]{1,3,2,0:T(8,128)(2,1)S(1)} fusion(bf16[4,1024,4,16]{1,3,2,0:T(8,128)(2,1)} %collective-permute-done.5, bf16[4,1024,4,32]{1,3,2,0:T(8,128)(2,1)S(1)} %constant_dynamic-update-slice_fusion.4, bf16[4,1024,4,16]{1,3,2,0:T(8,128)(2,1)} %collective-permute-done.4), kind=kLoop, calls=%fused_computation.20 | loop fusion | flops 6291456 | bytes 4194304 | tf_op jit(solution)/shard_map/concatenate | solution.py:21
  79.4 1.1 copy.144
  80.5 1.7 %reshape.559 = bf16[32,2,2048]{2,1,0:T(2,128)(2,1)} reshape(bf16[32,4,32,32]{3,2,1,0:T(8,128)(2,1)S(1)} %bitcast.344) | data formatting | bytes 524288
  82.2 11.3 %all-to-all-start.1 = ((bf16[32,2,2048]{2,1,0:T(2,128)(2,1)}), bf16[32,2,2048]{2,1,0:T(2,128)(2,1)S(1)}, u32[]{:S(2)}, u32[]{:S(2)}) async-start(bf16[32,2,2048]{2,1,0:T(2,128)(2,1)} %reshape.559), calls=%async_computation.1 | async-start | bytes 524288 | tf_op jit(solution)/shard_map/all_to_all | solution.py:154
  93.6 1.4 %pad_maximum_fusion = bf16[4,1024,4,64]{1,3,2,0:T(8,128)(2,1)S(1)} fusion(bf16[4,1024,4,16]{1,3,2,0:T(8,128)(2,1)} %collective-permute-done.1, bf16[4,1024,4,32]{1,3,2,0:T(8,128)(2,1)S(1)} %constant_dynamic-update-slice_fusion, bf16[4,1024,4,16]{1,3,2,0:T(8,128)(2,1)} %collective-permute-done), kind=kLoop, calls=%fused_computation.19 | loop fusion | flops 6291456 | bytes 4194304 | tf_op jit(solution)/shard_map/concatenate | solution.py:21
  97.4 1.7 %reshape.557 = bf16[32,2,2048]{2,1,0:T(2,128)(2,1)} reshape(bf16[32,4,32,32]{3,2,1,0:T(8,128)(2,1)S(1)} %bitcast.345) | data formatting | bytes 524288
  99.1 5.9 %all-to-all-done.1 = bf16[32,2,2048]{2,1,0:T(2,128)(2,1)S(1)} async-done(((bf16[32,2,2048]{2,1,0:T(2,128)(2,1)}), bf16[32,2,2048]{2,1,0:T(2,128)(2,1)S(1)}, u32[]{:S(2)}, u32[]{:S(2)}) %all-to-all-start.1) | async-done | bytes 262176 | tf_op jit(solution)/shard_map/all_to_all | solution.py:154
  105.0 4.9 %all-to-all-start = ((bf16[32,2,2048]{2,1,0:T(2,128)(2,1)}), bf16[32,2,2048]{2,1,0:T(2,128)(2,1)S(1)}, u32[]{:S(2)}, u32[]{:S(2)}) async-start(bf16[32,2,2048]{2,1,0:T(2,128)(2,1)} %reshape.557), calls=%async_computation | async-start | bytes 524288 | tf_op jit(solution)/shard_map/all_to_all | solution.py:154
  112.3 3.5 %collective-permute-start.6 = (f32[16,4,32]{0,2,1:T(8,128)S(1)}, f32[16,4,32]{0,2,1:T(8,128)S(1)}, u32[]{:S(2)}, u32[]{:S(2)}) collective-permute-start(f32[16,4,32]{0,2,1:T(8,128)S(1)} %get-tuple-element.145), channel_id=1, source_target_pairs={{0,8},{8,16},{16,24},{24,32},{32,40},{40,48},{48,56},{56,64},{64,7... | collective-permute-start | bytes 24584 | tf_op jit(solution)/shard_map/ppermute | solution.py:19
  115.9 1.9 %collective-permute-start.7 = (f32[16,4,32]{0,2,1:T(8,128)S(1)}, f32[16,4,32]{0,2,1:T(8,128)S(1)}, u32[]{:S(2)}, u32[]{:S(2)}) collective-permute-start(f32[16,4,32]{0,2,1:T(8,128)S(1)} %get-tuple-element.146), channel_id=1, source_target_pairs={{8,0},{16,8},{24,16},{32,24},{40,32},{48,40},{56,48},{64,56},{72,6... | collective-permute-start | bytes 24584 | tf_op jit(solution)/shard_map/ppermute | solution.py:20
  117.9 3.6 %all-to-all-done = bf16[32,2,2048]{2,1,0:T(2,128)(2,1)S(1)} async-done(((bf16[32,2,2048]{2,1,0:T(2,128)(2,1)}), bf16[32,2,2048]{2,1,0:T(2,128)(2,1)S(1)}, u32[]{:S(2)}, u32[]{:S(2)}) %all-to-all-start) | async-done | bytes 262176 | tf_op jit(solution)/shard_map/all_to_all | solution.py:154
  124.0 4.5 %collective-permute-start.2 = (f32[16,4,32]{0,2,1:T(8,128)S(1)}, f32[16,4,32]{0,2,1:T(8,128)S(1)}, u32[]{:S(2)}, u32[]{:S(2)}) collective-permute-start(f32[16,4,32]{0,2,1:T(8,128)S(1)} %get-tuple-element.143), channel_id=1, source_target_pairs={{0,8},{8,16},{16,24},{24,32},{32,40},{40,48},{48,56},{56,64},{64,7... | collective-permute-start | bytes 24584 | tf_op jit(solution)/shard_map/ppermute | solution.py:19
  128.5 1.9 %collective-permute-start.3 = (f32[16,4,32]{0,2,1:T(8,128)S(1)}, f32[16,4,32]{0,2,1:T(8,128)S(1)}, u32[]{:S(2)}, u32[]{:S(2)}) collective-permute-start(f32[16,4,32]{0,2,1:T(8,128)S(1)} %get-tuple-element.144), channel_id=1, source_target_pairs={{8,0},{16,8},{24,16},{32,24},{40,32},{48,40},{56,48},{64,56},{72,6... | collective-permute-start | bytes 24584 | tf_op jit(solution)/shard_map/ppermute | solution.py:20
  130.9 3.1 %collective-permute-done.3 = f32[16,4,32]{0,2,1:T(8,128)S(1)} collective-permute-done((f32[16,4,32]{0,2,1:T(8,128)S(1)}, f32[16,4,32]{0,2,1:T(8,128)S(1)}, u32[]{:S(2)}, u32[]{:S(2)}) %collective-permute-start.3) | collective-permute-done | bytes 8224 | tf_op jit(solution)/shard_map/ppermute | solution.py:20
  (207 shorter events, 42.9 us)
Async XLA Ops:
  33.7 0.9 copy-start
  36.0 0.9 copy-start.2
  37.4 0.9 copy-start.3
  38.8 0.9 copy-start.5
  39.8 11.5 %copy-start.1 = (bf16[4,32,8,384]{3,1,2,0:T(8,128)(2,1)S(1)}, bf16[4,32,8,384]{3,1,2,0:T(8,128)(2,1)}, u32[]{:S(2)}) copy-start(bf16[4,32,8,384]{3,1,2,0:T(8,128)(2,1)} %copy-done) | copy-start | bytes 2359300
  41.1 34.9 %collective-permute-start.4 = (bf16[4,1024,4,16]{1,3,2,0:T(8,128)(2,1)}, bf16[4,1024,4,16]{1,3,2,0:T(8,128)(2,1)}, u32[]{:S(2)}, u32[]{:S(2)}) collective-permute-start(bf16[4,1024,4,16]{1,3,2,0:T(8,128)(2,1)} %get-tuple-element.121), channel_id=1, source_target_pairs={{0,1},{1,2},{2,3},{3,4},{4,5},{5,6},{6,7},{8,9},{9,10},{10,11},{11... | collective-permute-start | bytes 1572872 | tf_op jit(solution)/shard_map/ppermute | solution.py:19
  45.7 30.3 %collective-permute-start.5 = (bf16[4,1024,4,16]{1,3,2,0:T(8,128)(2,1)}, bf16[4,1024,4,16]{1,3,2,0:T(8,128)(2,1)}, u32[]{:S(2)}, u32[]{:S(2)}) collective-permute-start(bf16[4,1024,4,16]{1,3,2,0:T(8,128)(2,1)} %get-tuple-element.122), channel_id=1, source_target_pairs={{1,0},{2,1},{3,2},{4,3},{5,4},{6,5},{7,6},{9,8},{10,9},{11,10},{12... | collective-permute-start | bytes 1572872 | tf_op jit(solution)/shard_map/ppermute | solution.py:20
  52.4 2.3 %copy-start.4 = (bf16[4,32,8,384]{3,1,2,0:T(8,128)(2,1)S(1)}, bf16[4,32,8,384]{3,1,2,0:T(8,128)(2,1)}, u32[]{:S(2)}) copy-start(bf16[4,32,8,384]{3,1,2,0:T(8,128)(2,1)} %copy-done.3) | copy-start | bytes 2359300
  59.2 34.4 %collective-permute-start = (bf16[4,1024,4,16]{1,3,2,0:T(8,128)(2,1)}, bf16[4,1024,4,16]{1,3,2,0:T(8,128)(2,1)}, u32[]{:S(2)}, u32[]{:S(2)}) collective-permute-start(bf16[4,1024,4,16]{1,3,2,0:T(8,128)(2,1)} %get-tuple-element.117), channel_id=1, source_target_pairs={{0,1},{1,2},{2,3},{3,4},{4,5},{5,6},{6,7},{8,9},{9,10},{10,11},{11... | collective-permute-start | bytes 1572872 | tf_op jit(solution)/shard_map/ppermute | solution.py:19
  62.9 30.7 %collective-permute-start.1 = (bf16[4,1024,4,16]{1,3,2,0:T(8,128)(2,1)}, bf16[4,1024,4,16]{1,3,2,0:T(8,128)(2,1)}, u32[]{:S(2)}, u32[]{:S(2)}) collective-permute-start(bf16[4,1024,4,16]{1,3,2,0:T(8,128)(2,1)} %get-tuple-element.118), channel_id=1, source_target_pairs={{1,0},{2,1},{3,2},{4,3},{5,4},{6,5},{7,6},{9,8},{10,9},{11,10},{12... | collective-permute-start | bytes 1572872 | tf_op jit(solution)/shard_map/ppermute | solution.py:20
  82.2 22.8 %all-to-all-start.1 = ((bf16[32,2,2048]{2,1,0:T(2,128)(2,1)}), bf16[32,2,2048]{2,1,0:T(2,128)(2,1)S(1)}, u32[]{:S(2)}, u32[]{:S(2)}) async-start(bf16[32,2,2048]{2,1,0:T(2,128)(2,1)} %reshape.559), calls=%async_computation.1 | async-start | bytes 524288 | tf_op jit(solution)/shard_map/all_to_all | solution.py:154
  105.0 16.4 %all-to-all-start = ((bf16[32,2,2048]{2,1,0:T(2,128)(2,1)}), bf16[32,2,2048]{2,1,0:T(2,128)(2,1)S(1)}, u32[]{:S(2)}, u32[]{:S(2)}) async-start(bf16[32,2,2048]{2,1,0:T(2,128)(2,1)} %reshape.557), calls=%async_computation | async-start | bytes 524288 | tf_op jit(solution)/shard_map/all_to_all | solution.py:154
  112.3 18.0 %collective-permute-start.6 = (f32[16,4,32]{0,2,1:T(8,128)S(1)}, f32[16,4,32]{0,2,1:T(8,128)S(1)}, u32[]{:S(2)}, u32[]{:S(2)}) collective-permute-start(f32[16,4,32]{0,2,1:T(8,128)S(1)} %get-tuple-element.145), channel_id=1, source_target_pairs={{0,8},{8,16},{16,24},{24,32},{32,40},{40,48},{48,56},{56,64},{64,7... | collective-permute-start | bytes 24584 | tf_op jit(solution)/shard_map/ppermute | solution.py:19
  115.9 14.5 %collective-permute-start.7 = (f32[16,4,32]{0,2,1:T(8,128)S(1)}, f32[16,4,32]{0,2,1:T(8,128)S(1)}, u32[]{:S(2)}, u32[]{:S(2)}) collective-permute-start(f32[16,4,32]{0,2,1:T(8,128)S(1)} %get-tuple-element.146), channel_id=1, source_target_pairs={{8,0},{16,8},{24,16},{32,24},{40,32},{48,40},{56,48},{64,56},{72,6... | collective-permute-start | bytes 24584 | tf_op jit(solution)/shard_map/ppermute | solution.py:20
  124.0 6.9 %collective-permute-start.2 = (f32[16,4,32]{0,2,1:T(8,128)S(1)}, f32[16,4,32]{0,2,1:T(8,128)S(1)}, u32[]{:S(2)}, u32[]{:S(2)}) collective-permute-start(f32[16,4,32]{0,2,1:T(8,128)S(1)} %get-tuple-element.143), channel_id=1, source_target_pairs={{0,8},{8,16},{16,24},{24,32},{32,40},{40,48},{48,56},{56,64},{64,7... | collective-permute-start | bytes 24584 | tf_op jit(solution)/shard_map/ppermute | solution.py:19
  128.5 5.6 %collective-permute-start.3 = (f32[16,4,32]{0,2,1:T(8,128)S(1)}, f32[16,4,32]{0,2,1:T(8,128)S(1)}, u32[]{:S(2)}, u32[]{:S(2)}) collective-permute-start(f32[16,4,32]{0,2,1:T(8,128)S(1)} %get-tuple-element.144), channel_id=1, source_target_pairs={{8,0},{16,8},{24,16},{32,24},{40,32},{48,40},{56,48},{64,56},{72,6... | collective-permute-start | bytes 24584 | tf_op jit(solution)/shard_map/ppermute | solution.py:20
where the time goes:
time: 137 us; the launch traced here: 135 us
  starting transfers between devices  43.7 us (32%)
  matrix products  22.1 us (16%)
  local copies, waits for them, and re-layouts  21.9 us (16%)
  other arithmetic  21.6 us (16%)
  waiting for transfers between devices  12.7 us (9%)
  between operations  12.7 us (9%)
    ppermute x4, starting transfers between devices, extended(): before = lax.ppermute(last, axis, up)  16.4 us
    all_to_all x2, starting transfers between devices, body(): lax.all_to_all(pieces.astype(jnp.bfloat16), 'depth', split_axis=0, concat...  16.3 us
    eq x16, other arithmetic, lookup(): low_hot = (low_part[None] == levels[:, None, None]).astype(jnp.bfloat16)  12.6 us
    ppermute x4, starting transfers between devices, extended(): after = lax.ppermute(first, axis, down)  11 us
    dot_general x16, matrix products, lookup(): jnp.einsum('chl,lgk->chgk', table, low_hot, preferred_element_type=jnp.fl...  10.1 us
    all_to_all x2, waiting for transfers between devices, body(): lax.all_to_all(pieces.astype(jnp.bfloat16), 'depth', split_axis=0, concat...  9.51 us
    dot_general x8, matrix products, shear_columns(): jnp.einsum('crbk,kj->bjcr', windows, tap_matrix, preferred_element_type=j...  9.04 us
    unnamed x30, local copies, waits for them, and re-layouts  6.24 us
  transfers between devices with their start and end apart: 10, of which 3 were waited for; matrix products, arithmetic and copies ran while one was open for 20% of the time, Pallas kernels for 0%

commit v1 on v0

v1 whole, which is shorter than its diff:
```python
import jax
import jax.numpy as jnp
from jax import lax
from jax.experimental import pallas as pl
from jax.experimental.pallas import tpu as pltpu
from jax.sharding import PartitionSpec as P

VIEWS = 2
HALO = 16
LANES = 128
CENTER = 64


def sinc(t):
    angle = jnp.where(t == 0.0, 1.0, jnp.pi * t)
    return jnp.where(t == 0.0, 1.0, jnp.sin(angle) / angle)


def lanczos(offset):
    return jnp.where(jnp.abs(offset) < 3.0, sinc(offset) * sinc(offset / 3.0), 0.0)


def iota(shape, dim):
    return lax.broadcasted_iota(jnp.int32, shape, dim)


def pairs(size, first):
    out = []
    for a in range(first, size - 1, 2):
        out += [(a, a + 1), (a + 1, a)]
    return out


def lane_pick(row, index):
    table = jnp.broadcast_to(row, index.shape)
    return jnp.take_along_axis(table, index, axis=1, mode="promise_in_bounds")


def shear_kernel(ids, view, tf, vol, got_a, got_b, out, classed, moved, picture):
    slab, rows, width = vol.shape
    blocks = width // LANES
    wide = rows + 2 * HALO
    depth_rank, band_rank = ids[0], ids[1]
    depth = slab * ids[2]
    height = rows * ids[3]

    codes = tf[...].astype(jnp.float32)
    opacity = codes[3:4] / (64.0 * depth.astype(jnp.float32))
    premult = codes[0:3] / 255.0 * opacity
    palette = jnp.concatenate([premult, opacity], axis=0).astype(jnp.bfloat16).astype(jnp.float32)

    which = iota((VIEWS * slab, LANES), 0)
    lane = iota((VIEWS * slab, LANES), 1)
    place = depth_rank * slab + which % slab
    taps = []
    for column in range(2):
        q = jnp.where(which < slab, view[0, column], view[1, column])
        num = q * (2 * place + 1 - depth)
        whole = num // (2 * depth)
        frac = (num - whole * (2 * depth)).astype(jnp.float32) / (2.0 * depth.astype(jnp.float32))
        taps.append(
            lanczos(frac - (lane - CENTER).astype(jnp.float32))
            .astype(jnp.bfloat16)
            .astype(jnp.float32)
        )

    def shift(v, s, column):
        num = view[v, column] * (2 * (depth_rank * slab + s) + 1 - depth)
        return num // (2 * depth)

    base_x = iota((2 * LANES, LANES), 0) - iota((2 * LANES, LANES), 1)
    shape_y = (4 * rows, 4 * wide)
    to = iota(shape_y, 0)
    frm = iota(shape_y, 1)
    even = band_rank % 2 == 0
    start_a = jnp.where(even, rows, -HALO)
    start_b = jnp.where(even, -HALO, rows)
    at = frm % wide
    local = jnp.where(
        at < rows,
        at,
        jnp.where(at < rows + HALO, at - rows + start_a, at - rows - HALO + start_b),
    )
    world = local + band_rank * rows
    fits = (to // rows == frm // wide) & (world >= 0) & (world < height)
    base_y = jnp.where(fits, local - to % rows + CENTER, -4 * LANES)

    for s in range(slab):
        voxels = jnp.concatenate(
            [vol[s], got_a[s].astype(jnp.int32), got_b[s].astype(jnp.int32)], axis=0
        )
        side = jnp.zeros((wide, CENTER), jnp.int32)
        voxels = jnp.concatenate([side, voxels, side], axis=1)
        for k in range(blocks + 1):
            code = voxels[:, k * LANES : (k + 1) * LANES]
            high = code >= LANES
            low = code & (LANES - 1)
            for c in range(4):
                value = jnp.where(
                    high,
                    lane_pick(palette[c : c + 1, LANES:], low),
                    lane_pick(palette[c : c + 1, :LANES], low),
                )
                if k == 0:
                    value = jnp.where(iota(value.shape, 1) >= CENTER, value, 0.0)
                if k == blocks:
                    value = jnp.where(iota(value.shape, 1) < CENTER, value, 0.0)
                classed[c * wide : (c + 1) * wide, k * LANES : (k + 1) * LANES] = value.astype(
                    jnp.bfloat16
                )
        weights = jnp.concatenate(
            [
                lane_pick(
                    taps[0][v * slab + s : v * slab + s + 1],
                    jnp.clip(base_x - shift(v, s, 0), 0, LANES - 1),
                ).astype(jnp.bfloat16)
                for v in range(VIEWS)
            ],
            axis=1,
        )
        for k in range(blocks):
            part = jnp.dot(
                classed[:, k * LANES : (k + 2) * LANES],
                weights,
                preferred_element_type=jnp.float32,
            ).astype(jnp.bfloat16)
            for v in range(VIEWS):
                moved[v, :, k * LANES : (k + 1) * LANES] = part[:, v * LANES : (v + 1) * LANES]
        for v in range(VIEWS):
            index = jnp.clip(base_y - shift(v, s, 1), 0, LANES - 1)
            row = taps[1][v * slab + s : v * slab + s + 1]
            weights = jnp.concatenate(
                [
                    lane_pick(row, index[:, j * LANES : (j + 1) * LANES]).astype(jnp.bfloat16)
                    for j in range(4 * wide // LANES)
                ],
                axis=1,
            )
            facing = view[v, 3] >= 0
            for k in range(0, width, 256):
                sheared = jnp.dot(
                    weights, moved[v, :, k : k + 256], preferred_element_type=jnp.float32
                )
                if s == 0:
                    picture[v, :, k : k + 256] = sheared
                    continue
                before = picture[v, :, k : k + 256]
                front = jnp.where(facing, before, sheared)
                back = jnp.where(facing, sheared, before)
                through = 1.0 - front[3 * rows :]
                picture[v, :, k : k + 256] = front + jnp.concatenate([through] * 4, axis=0) * back
    strips = out.shape[0]
    strip = width // strips
    for v in range(VIEWS):
        for k in range(blocks):
            turned = picture[v, :, k * LANES : (k + 1) * LANES].T.astype(jnp.bfloat16)
            per = LANES // strip
            out[k * per : (k + 1) * per, v * strip : (v + 1) * strip, :] = turned.reshape(
                per, strip, 4 * rows
            )


def gather_kernel(ids, view, arrived, strip_out, send_a, send_b):
    slabs, both, lanes = arrived.shape
    strip = both // VIEWS
    rows = lanes // 4
    pick = 3 * rows + iota((strip, lanes), 1) % rows
    even = ids[0] % 2 == 0
    for v in range(VIEWS):
        facing = view[v, 3] >= 0
        picture = jnp.zeros((strip, lanes), jnp.float32)
        through = jnp.ones((strip, lanes), jnp.float32)
        for k in range(slabs):
            at = jnp.where(facing, k, slabs - 1 - k)
            part = arrived[at, v * strip : (v + 1) * strip, :].astype(jnp.float32)
            picture = picture + through * part
            through = through * (
                1.0 - jnp.take_along_axis(part, pick, axis=1, mode="promise_in_bounds")
            )
        strip_out[v] = picture
        first = picture[:HALO]
        last = picture[strip - HALO :]
        send_a[v] = jnp.where(even, last, first)
        send_b[v] = jnp.where(even, first, last)


def warp_kernel(ids, view, strip_in, got_a, got_b, out):
    strip, lanes = strip_in.shape[1:]
    width = strip * ids[2]
    even = ids[0] % 2 == 0
    shape = (strip, strip + 2 * HALO)
    start_a = jnp.where(even, strip, -HALO)
    start_b = jnp.where(even, -HALO, strip)
    at = iota(shape, 1)
    local = jnp.where(
        at < strip,
        at,
        jnp.where(at < strip + HALO, at - strip + start_a, at - strip - HALO + start_b),
    )
    column = iota(shape, 0)
    for v in range(VIEWS):
        num = view[v, 2] * (2 * (ids[0] * strip + column) + 1 - width) + width
        whole = num // (2 * width)
        frac = (num - whole * (2 * width)).astype(jnp.float32) / (2.0 * width.astype(jnp.float32))
        weights = lanczos(frac - (local - column - whole).astype(jnp.float32))
        source = jnp.concatenate([strip_in[v], got_a[v], got_b[v]], axis=0)
        out[v] = jnp.dot(
            weights,
            source,
            precision=lax.Precision.HIGHEST,
            preferred_element_type=jnp.float32,
        )


def call(kernel, outs, scratch=(), vmem_from=2):
    def run(*args):
        return pl.pallas_call(
            kernel,
            out_shape=outs,
            in_specs=[pl.BlockSpec(memory_space=pltpu.SMEM)] * vmem_from
            + [pl.BlockSpec(memory_space=pltpu.VMEM)] * (len(args) - vmem_from),
            out_specs=jax.tree.map(lambda _: pl.BlockSpec(memory_space=pltpu.VMEM), outs),
            scratch_shapes=list(scratch),
        )(*args)

    return run


def body(volume, tf_table, view_code):
    slab, rows, width = volume.shape
    depth_size = lax.axis_size("depth")
    band_size = lax.axis_size("band")
    depth_rank = lax.axis_index("depth")
    band_rank = lax.axis_index("band")
    strip = width // depth_size
    wide = rows + 2 * HALO
    lanes = 4 * rows
    ids = jnp.stack(
        [depth_rank, band_rank, jnp.int32(depth_size), jnp.int32(band_size)]
    ).astype(jnp.int32)
    even = band_rank % 2 == 0
    first = volume[:, :HALO]
    last = volume[:, rows - HALO :]
    got_a = lax.ppermute(
        jnp.where(even, last, first).astype(jnp.bfloat16), "band", pairs(band_size, 0)
    )
    got_b = lax.ppermute(
        jnp.where(even, first, last).astype(jnp.bfloat16), "band", pairs(band_size, 1)
    )
    pieces = call(
        shear_kernel,
        jax.ShapeDtypeStruct((depth_size, VIEWS * strip, lanes), jnp.bfloat16),
        (
            pltpu.VMEM((4 * wide, width + LANES), jnp.bfloat16),
            pltpu.VMEM((VIEWS, 4 * wide, width), jnp.bfloat16),
            pltpu.VMEM((VIEWS, lanes, width), jnp.float32),
        ),
    )(ids, view_code, tf_table, volume, got_a, got_b)
    arrived = lax.all_to_all(pieces, "depth", split_axis=0, concat_axis=0, tiled=True)
    edge = jax.ShapeDtypeStruct((VIEWS, HALO, lanes), jnp.float32)
    whole = jax.ShapeDtypeStruct((VIEWS, strip, lanes), jnp.float32)
    middle, send_a, send_b = call(gather_kernel, (whole, edge, edge))(ids, view_code, arrived)
    side_a = lax.ppermute(send_a, "depth", pairs(depth_size, 0))
    side_b = lax.ppermute(send_b, "depth", pairs(depth_size, 1))
    final = call(warp_kernel, whole)(ids, view_code, middle, side_a, side_b)
    return final.reshape(VIEWS, strip, 4, rows)


def solution(mesh):
    placed = (P("depth", "band", None), P(), P())
    return jax.shard_map(
        body, mesh=mesh, in_specs=placed, out_specs=P(None, "depth", None, "band"), check_vma=False
    )
```

time: 137 us -> 63.6 us (0.46)
  the two profiles are of different devices: /device:TPU:9 before, /device:TPU:3 now
where the time goes in v1:
time: 63.6 us; the launch traced here: 63.2 us
  blocking collectives  28.1 us (44%)
  Pallas kernels  12.1 us (19%)
  starting transfers between devices  9.36 us (15%)
  waiting for transfers between devices  9.04 us (14%)
  local copies, waits for them, and re-layouts  2.78 us (4%)
  other arithmetic  1.69 us (3%)
    all_to_all x1, blocking collectives, body(): lax.all_to_all(pieces, 'depth', split_axis=0, concat_axis=0, tiled=True)  28.1 us
    pallas_call x3, Pallas kernels, run(): pl.pallas_call(kernel, out_shape=outs, in_specs=[pl.BlockSpec(memory_spac...  12.1 us
    ppermute x1, starting transfers between devices, body(): lax.ppermute(jnp.where(even, last, first).astype(jnp.bfloat16), 'band', p...  5.31 us
    ppermute x1, waiting for transfers between devices, body(): lax.ppermute(jnp.where(even, last, first).astype(jnp.bfloat16), 'band', p...  4.99 us
    ppermute x1, waiting for transfers between devices, body(): side_b = lax.ppermute(send_b, 'depth', pairs(depth_size, 1))  4.04 us
    ppermute x1, starting transfers between devices, body(): side_b = lax.ppermute(send_b, 'depth', pairs(depth_size, 1))  2.09 us
    reshape x1, local copies, waits for them, and re-layouts, body(): return final.reshape(VIEWS, strip, 4, rows)  1.53 us
    ppermute x1, starting transfers between devices, body(): side_a = lax.ppermute(send_a, 'depth', pairs(depth_size, 0))  1.29 us
  transfers between devices with their start and end apart: 4, of which 2 were waited for; matrix products, arithmetic and copies ran while one was open for 1% of the time, Pallas kernels for 0%

profile of v1, /device:TPU:3, one launch (start us, length us, event | category | flops | bytes accessed | tf_op | source)
XLA Modules:
  0.0 63.2 jit_solution(2690320822961452448)
XLA Ops:
  0.0 1.1 %select_convert_fusion = (bf16[4,16,1024]{2,1,0:T(8,128)(2,1)S(1)}, bf16[4,16,1024]{2,1,0:T(8,128)(2,1)S(1)}) fusion(s32[4,32,1024]{2,1,0:T(8,128)} %vol.1, pred[]{:T(512)S(6)} %eq.5), kind=kLoop, calls=%fused_computation | loop fusion | flops 262144 | bytes 786433 | tf_op jit(solution)/shard_map/convert_element_type | solution.py:248
  1.1 0.7 %collective-permute-start.1 = (bf16[4,16,1024]{2,1,0:T(8,128)(2,1)S(1)}, bf16[4,16,1024]{2,1,0:T(8,128)(2,1)S(1)}, u32[]{:S(2)}, u32[]{:S(2)}) collective-permute-start(bf16[4,16,1024]{2,1,0:T(8,128)(2,1)S(1)} %get-tuple-element.11), channel_id=1, source_target_pairs={{1,2},{2,1},{3,4},{4,3},{5,6},{6,5},{9,10},{10,9},{11,12},{12,11},... | collective-permute-start | bytes 393224 | tf_op jit(solution)/shard_map/ppermute | solution.py:247
  1.8 5.3 %collective-permute-start = (bf16[4,16,1024]{2,1,0:T(8,128)(2,1)S(1)}, bf16[4,16,1024]{2,1,0:T(8,128)(2,1)S(1)}, u32[]{:S(2)}, u32[]{:S(2)}) collective-permute-start(bf16[4,16,1024]{2,1,0:T(8,128)(2,1)S(1)} %get-tuple-element.12), channel_id=1, source_target_pairs={{0,1},{1,0},{2,3},{3,2},{4,5},{5,4},{6,7},{7,6},{8,9},{9,8},{10,11... | collective-permute-start | bytes 393224 | tf_op jit(solution)/shard_map/ppermute | solution.py:244
  7.1 0.6 pad_add_fusion.ids
  7.7 0.0 collective-permute-done.1.got_b
  7.7 0.0 copy-start
  7.7 5.0 %collective-permute-done.got_a = bf16[4,16,1024]{2,1,0:T(8,128)(2,1)S(1)} collective-permute-done((bf16[4,16,1024]{2,1,0:T(8,128)(2,1)S(1)}, bf16[4,16,1024]{2,1,0:T(8,128)(2,1)S(1)}, u32[]{:S(2)}, u32[]{:S(2)}) %collective-permute-start) | collective-permute-done | bytes 131104 | tf_op jit(solution)/shard_map/ppermute | solution.py:244
  12.7 0.0 copy-done
  12.7 0.0 copy-start.1
  12.7 0.7 %copy-done.1 = bf16[4,16,1024]{2,1,0:T(8,128)(2,1)} copy-done((bf16[4,16,1024]{2,1,0:T(8,128)(2,1)}, bf16[4,16,1024]{2,1,0:T(8,128)(2,1)S(1)}, u32[]{:S(2)}) %copy-start.1) | copy-done | bytes 131096
  13.3 7.9 %shard_map.37 = bf16[32,64,128]{2,1,0:T(8,128)(2,1)} custom-call(s32[4]{0:T(128)} %pad_add_fusion.ids, s32[2,4]{1,0:T(2,128)} %view.5, s32[4,256]{1,0:T(4,128)} %tf.1, s32[4,32,1024]{2,1,0:T(8,128)} %vol.1, bf16[4,16,1024]{2,1,0:T(8,128)(2,1)} %copy-done.1, bf16[4,16,1024]{2,1,0:T(8,128)(2,1)} %copy-done), custom_call_target="tpu_custom_call" | custom-call | tf_op jit(solution)/shard_map/pallas_call | solution.py:217
  21.3 28.1 %all_to_all.5.arrived = bf16[32,64,128]{2,1,0:T(8,128)(2,1)} all-to-all(bf16[32,64,128]{2,1,0:T(8,128)(2,1)} %shard_map.37), channel_id=1, replica_groups=mesh['depth'=32,'band'=8] {'depth'}, dimensions={0} | all-to-all | bytes 1048576 | tf_op jit(solution)/shard_map/all_to_all | solution.py:259
  49.4 2.0 %shard_map.38 = (f32[2,32,128]{2,1,0:T(8,128)}, f32[2,16,128]{2,1,0:T(8,128)}, f32[2,16,128]{2,1,0:T(8,128)}) custom-call(s32[4]{0:T(128)} %pad_add_fusion.ids, s32[2,4]{1,0:T(2,128)} %view.5, bf16[32,64,128]{2,1,0:T(8,128)(2,1)} %all_to_all.5.arrived), custom_call_target="tpu_custom_call" | custom-call | tf_op jit(solution)/shard_map/pallas_call | solution.py:217
  51.3 1.3 %collective-permute-start.2 = (f32[2,16,128]{2,1,0:T(8,128)}, f32[2,16,128]{2,1,0:T(8,128)S(1)}, u32[]{:S(2)}, u32[]{:S(2)}) collective-permute-start(f32[2,16,128]{2,1,0:T(8,128)} %get-tuple-element.9), channel_id=1, source_target_pairs={{0,8},{8,0},{16,24},{24,16},{32,40},{40,32},{48,56},{56,48},{64,72... | collective-permute-start | bytes 49160 | tf_op jit(solution)/shard_map/ppermute | solution.py:263
  52.6 2.1 %collective-permute-start.3 = (f32[2,16,128]{2,1,0:T(8,128)}, f32[2,16,128]{2,1,0:T(8,128)S(1)}, u32[]{:S(2)}, u32[]{:S(2)}) collective-permute-start(f32[2,16,128]{2,1,0:T(8,128)} %get-tuple-element.10), channel_id=1, source_target_pairs={{8,16},{16,8},{24,32},{32,24},{40,48},{48,40},{56,64},{64,56},{72,... | collective-permute-start | bytes 49160 | tf_op jit(solution)/shard_map/ppermute | solution.py:264
  54.7 0.0 collective-permute-done.2.got_a
  54.7 0.0 copy-start.2
  54.7 4.0 %collective-permute-done.3.got_b = f32[2,16,128]{2,1,0:T(8,128)S(1)} collective-permute-done((f32[2,16,128]{2,1,0:T(8,128)}, f32[2,16,128]{2,1,0:T(8,128)S(1)}, u32[]{:S(2)}, u32[]{:S(2)}) %collective-permute-start.3) | collective-permute-done | bytes 16416 | tf_op jit(solution)/shard_map/ppermute | solution.py:264
  58.8 0.0 copy-start.3
  58.8 0.0 copy-done.2
  58.8 0.6 copy-done.3
  59.4 2.3 %shard_map.39 = f32[2,32,128]{2,1,0:T(8,128)} custom-call(s32[4]{0:T(128)} %pad_add_fusion.ids, s32[2,4]{1,0:T(2,128)} %view.5, f32[2,32,128]{2,1,0:T(8,128)} %get-tuple-element.8.strip_in, f32[2,16,128]{2,1,0:T(8,128)} %copy-done.2, f32[2,16,128]{2,1,0:T(8,128)} %copy-done.3), custom_call_target="tpu_custom_call" | custom-call | tf_op jit(solution)/shard_map/pallas_call | solution.py:217
  61.6 1.5 %reshape.3 = f32[2,32,4,32]{3,2,1,0:T(4,128)} reshape(f32[2,32,128]{2,1,0:T(8,128)} %shard_map.39) | data formatting | bytes 65536 | tf_op jit(solution)/shard_map/reshape | solution.py:266
Async XLA Ops:
  1.1 6.6 %collective-permute-start.1 = (bf16[4,16,1024]{2,1,0:T(8,128)(2,1)S(1)}, bf16[4,16,1024]{2,1,0:T(8,128)(2,1)S(1)}, u32[]{:S(2)}, u32[]{:S(2)}) collective-permute-start(bf16[4,16,1024]{2,1,0:T(8,128)(2,1)S(1)} %get-tuple-element.11), channel_id=1, source_target_pairs={{1,2},{2,1},{3,4},{4,3},{5,6},{6,5},{9,10},{10,9},{11,12},{12,11},... | collective-permute-start | bytes 393224 | tf_op jit(solution)/shard_map/ppermute | solution.py:247
  1.8 10.9 %collective-permute-start = (bf16[4,16,1024]{2,1,0:T(8,128)(2,1)S(1)}, bf16[4,16,1024]{2,1,0:T(8,128)(2,1)S(1)}, u32[]{:S(2)}, u32[]{:S(2)}) collective-permute-start(bf16[4,16,1024]{2,1,0:T(8,128)(2,1)S(1)} %get-tuple-element.12), channel_id=1, source_target_pairs={{0,1},{1,0},{2,3},{3,2},{4,5},{5,4},{6,7},{7,6},{8,9},{9,8},{10,11... | collective-permute-start | bytes 393224 | tf_op jit(solution)/shard_map/ppermute | solution.py:244
  7.7 5.0 %copy-start = (bf16[4,16,1024]{2,1,0:T(8,128)(2,1)}, bf16[4,16,1024]{2,1,0:T(8,128)(2,1)S(1)}, u32[]{:S(2)}) copy-start(bf16[4,16,1024]{2,1,0:T(8,128)(2,1)S(1)} %collective-permute-done.1.got_b) | copy-start | bytes 393220
  12.7 0.7 %copy-start.1 = (bf16[4,16,1024]{2,1,0:T(8,128)(2,1)}, bf16[4,16,1024]{2,1,0:T(8,128)(2,1)S(1)}, u32[]{:S(2)}) copy-start(bf16[4,16,1024]{2,1,0:T(8,128)(2,1)S(1)} %collective-permute-done.got_a) | copy-start | bytes 393220
  51.3 3.4 %collective-permute-start.2 = (f32[2,16,128]{2,1,0:T(8,128)}, f32[2,16,128]{2,1,0:T(8,128)S(1)}, u32[]{:S(2)}, u32[]{:S(2)}) collective-permute-start(f32[2,16,128]{2,1,0:T(8,128)} %get-tuple-element.9), channel_id=1, source_target_pairs={{0,8},{8,0},{16,24},{24,16},{32,40},{40,32},{48,56},{56,48},{64,72... | collective-permute-start | bytes 49160 | tf_op jit(solution)/shard_map/ppermute | solution.py:263
  52.6 6.2 %collective-permute-start.3 = (f32[2,16,128]{2,1,0:T(8,128)}, f32[2,16,128]{2,1,0:T(8,128)S(1)}, u32[]{:S(2)}, u32[]{:S(2)}) collective-permute-start(f32[2,16,128]{2,1,0:T(8,128)} %get-tuple-element.10), channel_id=1, source_target_pairs={{8,16},{16,8},{24,32},{32,24},{40,48},{48,40},{56,64},{64,56},{72,... | collective-permute-start | bytes 49160 | tf_op jit(solution)/shard_map/ppermute | solution.py:264
  54.7 4.1 %copy-start.2 = (f32[2,16,128]{2,1,0:T(8,128)}, f32[2,16,128]{2,1,0:T(8,128)S(1)}, u32[]{:S(2)}) copy-start(f32[2,16,128]{2,1,0:T(8,128)S(1)} %collective-permute-done.2.got_a) | copy-start | bytes 49156
  58.8 0.6 copy-start.3

commit v2 on v1

--- a/solution.py
+++ b/solution.py
@@ -9,6 +9,7 @@
 HALO = 16
 LANES = 128
 CENTER = 64
+VMEM_LIMIT = 16 * 2**20
 
 
 def sinc(t):
@@ -221,6 +222,7 @@
             + [pl.BlockSpec(memory_space=pltpu.VMEM)] * (len(args) - vmem_from),
             out_specs=jax.tree.map(lambda _: pl.BlockSpec(memory_space=pltpu.VMEM), outs),
             scratch_shapes=list(scratch),
+            compiler_params=pltpu.CompilerParams(vmem_limit_bytes=VMEM_LIMIT),
         )(*args)
 
     return run

time: 63.6 us -> 57.6 us (0.906)
  the two profiles are of different devices: /device:TPU:3 before, /device:TPU:11 now
where the time goes in v2:
time: 57.6 us; the launch traced here: 57.4 us
  blocking collectives  27.8 us (48%)
  starting transfers between devices  9.47 us (16%)
  waiting for transfers between devices  9.35 us (16%)
  Pallas kernels  8.77 us (15%)
  other arithmetic  1.21 us (2%)
  local copies, waits for them, and re-layouts  0.8 us (1%)
    all_to_all x1, blocking collectives, body(): lax.all_to_all(pieces, 'depth', split_axis=0, concat_axis=0, tiled=True)  27.8 us
    pallas_call x3, Pallas kernels, run(): pl.pallas_call(kernel, out_shape=outs, in_specs=[pl.BlockSpec(memory_spac...  8.77 us
    ppermute x1, waiting for transfers between devices, body(): side_b = lax.ppermute(send_b, 'depth', pairs(depth_size, 1))  3.82 us
    ppermute x1, starting transfers between devices, body(): lax.ppermute(jnp.where(even, first, last).astype(jnp.bfloat16), 'band', p...  3.64 us
    ppermute x1, waiting for transfers between devices, body(): lax.ppermute(jnp.where(even, last, first).astype(jnp.bfloat16), 'band', p...  2.92 us
    ppermute x1, waiting for transfers between devices, body(): lax.ppermute(jnp.where(even, first, last).astype(jnp.bfloat16), 'band', p...  2.61 us
    ppermute x1, starting transfers between devices, body(): lax.ppermute(jnp.where(even, last, first).astype(jnp.bfloat16), 'band', p...  2.34 us
    ppermute x1, starting transfers between devices, body(): side_b = lax.ppermute(send_b, 'depth', pairs(depth_size, 1))  2.11 us
  transfers between devices with their start and end apart: 4, of which 3 were waited for; matrix products, arithmetic and copies ran while one was open for 0% of the time, Pallas kernels for 0%

profile of v2, /device:TPU:11, one launch (start us, length us, event | category | flops | bytes accessed | tf_op | source)
XLA Modules:
  0.0 57.4 jit_solution(13675936459869126324)
XLA Ops:
  0.0 0.0 copy-start
  0.0 1.1 %select_convert_fusion = (bf16[4,16,1024]{2,1,0:T(8,128)(2,1)S(1)}, bf16[4,16,1024]{2,1,0:T(8,128)(2,1)S(1)}) fusion(s32[4,32,1024]{2,1,0:T(8,128)} %vol.1, pred[]{:T(512)S(6)} %eq.5), kind=kLoop, calls=%fused_computation | loop fusion | flops 262144 | bytes 786433 | tf_op jit(solution)/shard_map/convert_element_type | solution.py:250
  1.1 3.6 %collective-permute-start.1 = (bf16[4,16,1024]{2,1,0:T(8,128)(2,1)S(1)}, bf16[4,16,1024]{2,1,0:T(8,128)(2,1)S(1)}, u32[]{:S(2)}, u32[]{:S(2)}) collective-permute-start(bf16[4,16,1024]{2,1,0:T(8,128)(2,1)S(1)} %get-tuple-element.11), channel_id=1, source_target_pairs={{1,2},{2,1},{3,4},{4,3},{5,6},{6,5},{9,10},{10,9},{11,12},{12,11},... | collective-permute-start | bytes 393224 | tf_op jit(solution)/shard_map/ppermute | solution.py:249
  4.8 2.3 %collective-permute-start = (bf16[4,16,1024]{2,1,0:T(8,128)(2,1)S(1)}, bf16[4,16,1024]{2,1,0:T(8,128)(2,1)S(1)}, u32[]{:S(2)}, u32[]{:S(2)}) collective-permute-start(bf16[4,16,1024]{2,1,0:T(8,128)(2,1)S(1)} %get-tuple-element.12), channel_id=1, source_target_pairs={{0,1},{1,0},{2,3},{3,2},{4,5},{5,4},{6,7},{7,6},{8,9},{9,8},{10,11... | collective-permute-start | bytes 393224 | tf_op jit(solution)/shard_map/ppermute | solution.py:246
  7.1 0.0 copy-start.2
  7.1 0.0 copy-start.1
  7.1 0.1 pad_add_fusion.ids
  7.2 2.6 %collective-permute-done.1.got_b = bf16[4,16,1024]{2,1,0:T(8,128)(2,1)S(1)} collective-permute-done((bf16[4,16,1024]{2,1,0:T(8,128)(2,1)S(1)}, bf16[4,16,1024]{2,1,0:T(8,128)(2,1)S(1)}, u32[]{:S(2)}, u32[]{:S(2)}) %collective-permute-start.1) | collective-permute-done | bytes 131104 | tf_op jit(solution)/shard_map/ppermute | solution.py:249
  9.8 2.9 %collective-permute-done.got_a = bf16[4,16,1024]{2,1,0:T(8,128)(2,1)S(1)} collective-permute-done((bf16[4,16,1024]{2,1,0:T(8,128)(2,1)S(1)}, bf16[4,16,1024]{2,1,0:T(8,128)(2,1)S(1)}, u32[]{:S(2)}, u32[]{:S(2)}) %collective-permute-start) | collective-permute-done | bytes 131104 | tf_op jit(solution)/shard_map/ppermute | solution.py:246
  12.7 0.0 copy-done
  12.8 0.0 copy-done.2
  12.8 0.0 copy-done.1
  12.8 6.6 %shard_map.37 = bf16[32,64,128]{2,1,0:T(8,128)(2,1)S(1)} custom-call(s32[4]{0:T(128)S(1)} %pad_add_fusion.ids, s32[2,4]{1,0:T(2,128)S(1)} %copy-done.1, s32[4,256]{1,0:T(4,128)S(1)} %copy-done.2, s32[4,32,1024]{2,1,0:T(8,128)S(1)} %copy-done, bf16[4,16,1024]{2,1,0:T(8,128)(2,1)S(1)} %collective-permute-done.got_a, ...), custom_call_target="tpu_custom_call" | custom-call | tf_op jit(solution)/shard_map/pallas_call | solution.py:218
  19.3 27.8 %all_to_all.5.arrived = bf16[32,64,128]{2,1,0:T(8,128)(2,1)S(1)} all-to-all(bf16[32,64,128]{2,1,0:T(8,128)(2,1)S(1)} %shard_map.37), channel_id=1, replica_groups=mesh['depth'=32,'band'=8] {'depth'}, dimensions={0} | all-to-all | bytes 1048576 | tf_op jit(solution)/shard_map/all_to_all | solution.py:261
  47.1 0.8 %shard_map.38 = (f32[2,32,128]{2,1,0:T(8,128)S(1)}, f32[2,16,128]{2,1,0:T(8,128)S(1)}, f32[2,16,128]{2,1,0:T(8,128)S(1)}) custom-call(s32[4]{0:T(128)S(1)} %pad_add_fusion.ids, s32[2,4]{1,0:T(2,128)S(1)} %copy-done.1, bf16[32,64,128]{2,1,0:T(8,128)(2,1)S(1)} %all_to_all.5.arrived), custom_call_target="tpu_custom_call" | custom-call | tf_op jit(solution)/shard_map/pallas_call | solution.py:218
  48.0 1.4 %collective-permute-start.2 = (f32[2,16,128]{2,1,0:T(8,128)S(1)}, f32[2,16,128]{2,1,0:T(8,128)S(1)}, u32[]{:S(2)}, u32[]{:S(2)}) collective-permute-start(f32[2,16,128]{2,1,0:T(8,128)S(1)} %get-tuple-element.9), channel_id=1, source_target_pairs={{0,8},{8,0},{16,24},{24,16},{32,40},{40,32},{48,56},{56,48},{64,72... | collective-permute-start | bytes 49160 | tf_op jit(solution)/shard_map/ppermute | solution.py:265
  49.3 2.1 %collective-permute-start.3 = (f32[2,16,128]{2,1,0:T(8,128)S(1)}, f32[2,16,128]{2,1,0:T(8,128)S(1)}, u32[]{:S(2)}, u32[]{:S(2)}) collective-permute-start(f32[2,16,128]{2,1,0:T(8,128)S(1)} %get-tuple-element.10), channel_id=1, source_target_pairs={{8,16},{16,8},{24,32},{32,24},{40,48},{48,40},{56,64},{64,56},{72,... | collective-permute-start | bytes 49160 | tf_op jit(solution)/shard_map/ppermute | solution.py:266
  51.5 0.0 collective-permute-done.2.got_a
  51.5 3.8 %collective-permute-done.3.got_b = f32[2,16,128]{2,1,0:T(8,128)S(1)} collective-permute-done((f32[2,16,128]{2,1,0:T(8,128)S(1)}, f32[2,16,128]{2,1,0:T(8,128)S(1)}, u32[]{:S(2)}, u32[]{:S(2)}) %collective-permute-start.3) | collective-permute-done | bytes 16416 | tf_op jit(solution)/shard_map/ppermute | solution.py:266
  55.3 1.4 %shard_map.39 = f32[2,32,128]{2,1,0:T(8,128)S(1)} custom-call(s32[4]{0:T(128)S(1)} %pad_add_fusion.ids, s32[2,4]{1,0:T(2,128)S(1)} %copy-done.1, f32[2,32,128]{2,1,0:T(8,128)S(1)} %get-tuple-element.8.strip_in, f32[2,16,128]{2,1,0:T(8,128)S(1)} %collective-permute-done.2.got_a, f32[2,16,128]{2,1,0:T(8,128)S(1)} %collective-permute-done.3.got_b), custom_call_target="tpu_custom_call" | custom-call | tf_op jit(solution)/shard_map/pallas_call | solution.py:218
  56.7 0.8 %reshape.3 = f32[2,32,4,32]{3,2,1,0:T(4,128)} reshape(f32[2,32,128]{2,1,0:T(8,128)S(1)} %shard_map.39) | data formatting | bytes 65536 | tf_op jit(solution)/shard_map/reshape | solution.py:268
Async XLA Ops:
  0.0 12.8 %copy-start = (s32[4,32,1024]{2,1,0:T(8,128)S(1)}, s32[4,32,1024]{2,1,0:T(8,128)}, u32[]{:S(2)}) copy-start(s32[4,32,1024]{2,1,0:T(8,128)} %vol.1) | copy-start | bytes 1572868
  1.1 8.7 %collective-permute-start.1 = (bf16[4,16,1024]{2,1,0:T(8,128)(2,1)S(1)}, bf16[4,16,1024]{2,1,0:T(8,128)(2,1)S(1)}, u32[]{:S(2)}, u32[]{:S(2)}) collective-permute-start(bf16[4,16,1024]{2,1,0:T(8,128)(2,1)S(1)} %get-tuple-element.11), channel_id=1, source_target_pairs={{1,2},{2,1},{3,4},{4,3},{5,6},{6,5},{9,10},{10,9},{11,12},{12,11},... | collective-permute-start | bytes 393224 | tf_op jit(solution)/shard_map/ppermute | solution.py:249
  4.8 8.0 %collective-permute-start = (bf16[4,16,1024]{2,1,0:T(8,128)(2,1)S(1)}, bf16[4,16,1024]{2,1,0:T(8,128)(2,1)S(1)}, u32[]{:S(2)}, u32[]{:S(2)}) collective-permute-start(bf16[4,16,1024]{2,1,0:T(8,128)(2,1)S(1)} %get-tuple-element.12), channel_id=1, source_target_pairs={{0,1},{1,0},{2,3},{3,2},{4,5},{5,4},{6,7},{7,6},{8,9},{9,8},{10,11... | collective-permute-start | bytes 393224 | tf_op jit(solution)/shard_map/ppermute | solution.py:246
  7.1 5.6 %copy-start.2 = (s32[4,256]{1,0:T(4,128)S(1)}, s32[4,256]{1,0:T(4,128)}, u32[]{:S(2)}) copy-start(s32[4,256]{1,0:T(4,128)} %tf.1) | copy-start | bytes 12292
  7.1 5.6 %copy-start.1 = (s32[2,4]{1,0:T(2,128)S(1)}, s32[2,4]{1,0:T(2,128)}, u32[]{:S(2)}) copy-start(s32[2,4]{1,0:T(2,128)} %view.5) | copy-start | bytes 100
  48.0 3.5 %collective-permute-start.2 = (f32[2,16,128]{2,1,0:T(8,128)S(1)}, f32[2,16,128]{2,1,0:T(8,128)S(1)}, u32[]{:S(2)}, u32[]{:S(2)}) collective-permute-start(f32[2,16,128]{2,1,0:T(8,128)S(1)} %get-tuple-element.9), channel_id=1, source_target_pairs={{0,8},{8,0},{16,24},{24,16},{32,40},{40,32},{48,56},{56,48},{64,72... | collective-permute-start | bytes 49160 | tf_op jit(solution)/shard_map/ppermute | solution.py:265
  49.3 5.9 %collective-permute-start.3 = (f32[2,16,128]{2,1,0:T(8,128)S(1)}, f32[2,16,128]{2,1,0:T(8,128)S(1)}, u32[]{:S(2)}, u32[]{:S(2)}) collective-permute-start(f32[2,16,128]{2,1,0:T(8,128)S(1)} %get-tuple-element.10), channel_id=1, source_target_pairs={{8,16},{16,8},{24,32},{32,24},{40,48},{48,40},{56,64},{64,56},{72,... | collective-permute-start | bytes 49160 | tf_op jit(solution)/shard_map/ppermute | solution.py:266

commit v3 on v2

v3 whole, which is shorter than its diff:
```python
import jax
import jax.numpy as jnp
from jax import lax
from jax.experimental import pallas as pl
from jax.experimental.pallas import tpu as pltpu
from jax.sharding import PartitionSpec as P

VIEWS = 2
HALO = 16
LANES = 128
CENTER = 64
VMEM_LIMIT = 16 * 2**20


def sinc(t):
    angle = jnp.where(t == 0.0, 1.0, jnp.pi * t)
    return jnp.where(t == 0.0, 1.0, jnp.sin(angle) / angle)


def lanczos(offset):
    return jnp.where(jnp.abs(offset) < 3.0, sinc(offset) * sinc(offset / 3.0), 0.0)


def iota(shape, dim):
    return lax.broadcasted_iota(jnp.int32, shape, dim)


def pairs(size, first):
    out = []
    for a in range(first, size - 1, 2):
        out += [(a, a + 1), (a + 1, a)]
    return out


def lane_pick(row, index):
    table = jnp.broadcast_to(row, index.shape)
    return jnp.take_along_axis(table, index, axis=1, mode="promise_in_bounds")


def classify(code, palette, out, k, last, group):
    high = code >= LANES
    low = code & (LANES - 1)
    for c in range(4):
        value = jnp.where(
            high,
            lane_pick(palette[c : c + 1, LANES:], low),
            lane_pick(palette[c : c + 1, :LANES], low),
        )
        if k == 0:
            value = jnp.where(iota(value.shape, 1) >= CENTER, value, 0.0)
        if k == last:
            value = jnp.where(iota(value.shape, 1) < CENTER, value, 0.0)
        out[c * group : (c + 1) * group, k * LANES : (k + 1) * LANES] = value.astype(jnp.bfloat16)


def shear_columns(voxels, palette, weights, classed, store):
    group, width = voxels.shape
    blocks = width // LANES
    side = jnp.zeros((group, CENTER), jnp.int32)
    voxels = jnp.concatenate([side, voxels, side], axis=1)
    for k in range(blocks + 1):
        classify(voxels[:, k * LANES : (k + 1) * LANES], palette, classed, k, blocks, group)
    for k in range(blocks):
        part = jnp.dot(
            classed[:, k * LANES : (k + 2) * LANES], weights, preferred_element_type=jnp.float32
        ).astype(jnp.bfloat16)
        for v in range(VIEWS):
            store(v, k, part[:, v * LANES : (v + 1) * LANES])


def own_kernel(ids, view, tf, vol, own, filter_x, filter_y, filter_w, palette_out, classed):
    slab, rows, width = vol.shape
    depth_rank, band_rank = ids[0], ids[1]
    depth = slab * ids[2]
    height = rows * ids[3]
    strip = filter_w.shape[1]

    codes = tf[...].astype(jnp.float32)
    opacity = codes[3:4] / (64.0 * depth.astype(jnp.float32))
    premult = codes[0:3] / 255.0 * opacity
    palette = jnp.concatenate([premult, opacity], axis=0).astype(jnp.bfloat16).astype(jnp.float32)
    palette_out[...] = palette

    which = iota((VIEWS * slab, LANES), 0)
    lane = iota((VIEWS * slab, LANES), 1)
    place = depth_rank * slab + which % slab
    taps = []
    for column in range(2):
        q = jnp.where(which < slab, view[0, column], view[1, column])
        num = q * (2 * place + 1 - depth)
        whole = num // (2 * depth)
        frac = (num - whole * (2 * depth)).astype(jnp.float32) / (2.0 * depth.astype(jnp.float32))
        taps.append(
            lanczos(frac - (lane - CENTER).astype(jnp.float32))
            .astype(jnp.bfloat16)
            .astype(jnp.float32)
        )

    def shift(v, s, column):
        num = view[v, column] * (2 * (depth_rank * slab + s) + 1 - depth)
        return num // (2 * depth)

    base_x = iota((2 * LANES, LANES), 0) - iota((2 * LANES, LANES), 1)
    for s in range(slab):
        for v in range(VIEWS):
            row = taps[0][v * slab + s : v * slab + s + 1]
            index = jnp.clip(base_x - shift(v, s, 0), 0, LANES - 1)
            filter_x[s, :, v * LANES : (v + 1) * LANES] = lane_pick(row, index).astype(jnp.bfloat16)

        def store(v, k, part):
            own[v, s, :, k * LANES : (k + 1) * LANES] = part

        shear_columns(vol[s], palette, filter_x[s], classed, store)

    lanes = 4 * rows
    to = iota((lanes, lanes), 0)
    frm = iota((lanes, lanes), 1)
    even = band_rank % 2 == 0
    start_a = jnp.where(even, rows, -HALO)
    start_b = jnp.where(even, -HALO, rows)
    at = frm % rows
    base_y = []
    for local in (at, jnp.where(at < HALO, at + start_a, at - HALO + start_b)):
        world = local + band_rank * rows
        fits = (to // rows == frm // rows) & (world >= 0) & (world < height)
        base_y.append(jnp.where(fits, local - to % rows + CENTER, -4 * LANES))
    for v in range(VIEWS):
        for s in range(slab):
            row = taps[1][v * slab + s : v * slab + s + 1]
            for j in range(2):
                index = jnp.clip(base_y[j] - shift(v, s, 1), 0, LANES - 1)
                filter_y[v, s, :, j * lanes : (j + 1) * lanes] = lane_pick(row, index).astype(
                    jnp.bfloat16
                )

    even = depth_rank % 2 == 0
    shape = (strip, strip + 2 * HALO)
    start_a = jnp.where(even, strip, -HALO)
    start_b = jnp.where(even, -HALO, strip)
    at = iota(shape, 1)
    local = jnp.where(
        at < strip,
        at,
        jnp.where(at < strip + HALO, at - strip + start_a, at - strip - HALO + start_b),
    )
    column = iota(shape, 0)
    for v in range(VIEWS):
        num = view[v, 2] * (2 * (depth_rank * strip + column) + 1 - width) + width
        whole = num // (2 * width)
        frac = (num - whole * (2 * width)).astype(jnp.float32) / (2.0 * width)
        filter_w[v] = lanczos(frac - (local - column - whole).astype(jnp.float32))


def slab_kernel(
    ids, view, palette, filter_x, filter_y, own, got_a, got_b, keep, send, classed, near
):
    slab = own.shape[1]
    lanes, width = own.shape[2:]
    rows = lanes // 4
    strip = keep.shape[1] // VIEWS
    for s in range(slab):

        def store(v, k, part):
            near[v, s, :, k * LANES : (k + 1) * LANES] = part

        voxels = jnp.concatenate(
            [got_a[s].astype(jnp.int32), got_b[s].astype(jnp.int32)], axis=0
        )
        shear_columns(voxels, palette[...], filter_x[s], classed, store)
    chunk = 2 * LANES
    per = chunk // (2 * strip)
    first = ids[0] % 2 == 0
    for v in range(VIEWS):
        facing = view[v, 3] >= 0
        for k in range(width // chunk):
            for step in range(slab):
                s = jnp.where(facing, step, slab - 1 - step)
                source = jnp.concatenate(
                    [
                        own[v, s, :, k * chunk : (k + 1) * chunk],
                        near[v, s, :, k * chunk : (k + 1) * chunk],
                    ],
                    axis=0,
                )
                sheared = jnp.dot(filter_y[v, s], source, preferred_element_type=jnp.float32)
                if step == 0:
                    picture = sheared
                    continue
                through = 1.0 - picture[3 * rows :]
                picture = picture + jnp.concatenate([through] * 4, axis=0) * sheared
            turned = picture.T.reshape(per, 2, strip, lanes)
            even, odd = turned[:, 0], turned[:, 1]
            at = slice(k * per, (k + 1) * per)
            keep[at, v * strip : (v + 1) * strip] = jnp.where(first, even, odd)
            send[at, v * strip : (v + 1) * strip] = jnp.where(first, odd, even).astype(
                jnp.bfloat16
            )


def merge_kernel(ids, view, keep, got, out):
    strips, both, lanes = keep.shape
    strip = both // VIEWS
    rows = lanes // 4
    first = ids[0] % 2 == 0
    pick = 3 * rows + iota((strip, lanes), 1) % rows
    for v in range(VIEWS):
        mine_front = (view[v, 3] >= 0) == first
        for k in range(strips):
            mine = keep[k, v * strip : (v + 1) * strip]
            other = got[k, v * strip : (v + 1) * strip].astype(jnp.float32)
            front = jnp.where(mine_front, mine, other)
            back = jnp.where(mine_front, other, mine)
            alpha = jnp.take_along_axis(front, pick, axis=1, mode="promise_in_bounds")
            out[k, v * strip : (v + 1) * strip] = (front + (1.0 - alpha) * back).astype(
                jnp.bfloat16
            )


def gather_kernel(ids, view, arrived, strip_out, send_a, send_b):
    slabs, both, lanes = arrived.shape
    strip = both // VIEWS
    rows = lanes // 4
    pick = 3 * rows + iota((strip, lanes), 1) % rows
    even = ids[0] % 2 == 0
    for v in range(VIEWS):
        facing = view[v, 3] >= 0
        picture = jnp.zeros((strip, lanes), jnp.float32)
        through = jnp.ones((strip, lanes), jnp.float32)
        for k in range(slabs):
            at = jnp.where(facing, k, slabs - 1 - k)
            part = arrived[at, v * strip : (v + 1) * strip, :].astype(jnp.float32)
            picture = picture + through * part
            through = through * (
                1.0 - jnp.take_along_axis(part, pick, axis=1, mode="promise_in_bounds")
            )
        strip_out[v] = picture
        first = picture[:HALO]
        last = picture[strip - HALO :]
        send_a[v] = jnp.where(even, last, first)
        send_b[v] = jnp.where(even, first, last)


def warp_kernel(filter_w, strip_in, got_a, got_b, out):
    rows = strip_in.shape[2] // 4
    for v in range(VIEWS):
        source = jnp.concatenate([strip_in[v], got_a[v], got_b[v]], axis=0)
        final = jnp.dot(
            filter_w[v],
            source,
            precision=lax.Precision.HIGHEST,
            preferred_element_type=jnp.float32,
        )
        for c in range(4):
            out[v, :, c, :] = final[:, c * rows : (c + 1) * rows]


def call(kernel, outs, scratch=(), vmem_from=2):
    def run(*args):
        return pl.pallas_call(
            kernel,
            out_shape=outs,
            in_specs=[pl.BlockSpec(memory_space=pltpu.SMEM)] * vmem_from
            + [pl.BlockSpec(memory_space=pltpu.VMEM)] * (len(args) - vmem_from),
            out_specs=jax.tree.map(lambda _: pl.BlockSpec(memory_space=pltpu.VMEM), outs),
            scratch_shapes=list(scratch),
            compiler_params=pltpu.CompilerParams(vmem_limit_bytes=VMEM_LIMIT),
        )(*args)

    return run


def body(volume, tf_table, view_code):
    slab, rows, width = volume.shape
    depth_size = lax.axis_size("depth")
    band_size = lax.axis_size("band")
    depth_rank = lax.axis_index("depth")
    band_rank = lax.axis_index("band")
    strip = width // depth_size
    lanes = 4 * rows
    bf16, f32 = jnp.bfloat16, jnp.float32
    ids = jnp.stack(
        [depth_rank, band_rank, jnp.int32(depth_size), jnp.int32(band_size)]
    ).astype(jnp.int32)
    even = band_rank % 2 == 0
    first = volume[:, :HALO]
    last = volume[:, rows - HALO :]
    got_a = lax.ppermute(jnp.where(even, last, first).astype(bf16), "band", pairs(band_size, 0))
    got_b = lax.ppermute(jnp.where(even, first, last).astype(bf16), "band", pairs(band_size, 1))
    own, filter_x, filter_y, filter_w, palette = call(
        own_kernel,
        (
            jax.ShapeDtypeStruct((VIEWS, slab, lanes, width), bf16),
            jax.ShapeDtypeStruct((slab, 2 * LANES, VIEWS * LANES), bf16),
            jax.ShapeDtypeStruct((VIEWS, slab, lanes, 2 * lanes), bf16),
            jax.ShapeDtypeStruct((VIEWS, strip, strip + 2 * HALO), f32),
            jax.ShapeDtypeStruct(tf_table.shape, f32),
        ),
        (pltpu.VMEM((lanes, width + LANES), bf16),),
    )(ids, view_code, tf_table, volume)
    half = (depth_size // 2, VIEWS * strip, lanes)
    keep, send = call(
        slab_kernel,
        (jax.ShapeDtypeStruct(half, f32), jax.ShapeDtypeStruct(half, bf16)),
        (
            pltpu.VMEM((8 * HALO, width + LANES), bf16),
            pltpu.VMEM((VIEWS, slab, 8 * HALO, width), bf16),
        ),
    )(ids, view_code, palette, filter_x, filter_y, own, got_a, got_b)
    got = lax.ppermute(send, "depth", pairs(depth_size, 0))
    merged = call(merge_kernel, jax.ShapeDtypeStruct(half, bf16))(ids, view_code, keep, got)
    arrived = lax.all_to_all(
        merged,
        "depth",
        split_axis=0,
        concat_axis=0,
        tiled=True,
        axis_index_groups=[list(range(i, depth_size, 2)) for i in range(2)],
    )
    edge = jax.ShapeDtypeStruct((VIEWS, HALO, lanes), f32)
    whole = jax.ShapeDtypeStruct((VIEWS, strip, lanes), f32)
    middle, send_a, send_b = call(gather_kernel, (whole, edge, edge))(ids, view_code, arrived)
    side_a = lax.ppermute(send_a, "depth", pairs(depth_size, 0))
    side_b = lax.ppermute(send_b, "depth", pairs(depth_size, 1))
    final = jax.ShapeDtypeStruct((VIEWS, strip, 4, rows), f32)
    return call(warp_kernel, final, (), 0)(filter_w, middle, side_a, side_b)


def solution(mesh):
    placed = (P("depth", "band", None), P(), P())
    return jax.shard_map(
        body, mesh=mesh, in_specs=placed, out_specs=P(None, "depth", None, "band"), check_vma=False
    )
```

time: 57.6 us -> 51.5 us (0.89)
  the two profiles are of different devices: /device:TPU:11 before, /device:TPU:1 now
where the time goes in v3:
time: 51.5 us; the launch traced here: 51.2 us
  blocking collectives  20 us (39%)
  starting transfers between devices  12.1 us (23%)
  Pallas kernels  11.3 us (22%)
  waiting for transfers between devices  4.21 us (8%)
  local copies, waits for them, and re-layouts  2.41 us (5%)
  other arithmetic  1.15 us (2%)
    all_to_all x1, blocking collectives, body(): lax.all_to_all(merged, 'depth', split_axis=0, concat_axis=0, tiled=True,...  20 us
    pallas_call x5, Pallas kernels, run(): pl.pallas_call(kernel, out_shape=outs, in_specs=[pl.BlockSpec(memory_spac...  11.3 us
    ppermute x1, starting transfers between devices, body(): lax.ppermute(jnp.where(even, last, first).astype(bf16), 'band', pairs(ban...  6.13 us
    ppermute x1, waiting for transfers between devices, body(): side_b = lax.ppermute(send_b, 'depth', pairs(depth_size, 1))  3.04 us
    unnamed x6, local copies, waits for them, and re-layouts  2.41 us
    ppermute x1, starting transfers between devices, body(): side_a = lax.ppermute(send_a, 'depth', pairs(depth_size, 0))  2.02 us
    ppermute x1, starting transfers between devices, body(): side_b = lax.ppermute(send_b, 'depth', pairs(depth_size, 1))  1.99 us
    ppermute x1, starting transfers between devices, body(): got = lax.ppermute(send, 'depth', pairs(depth_size, 0))  1.32 us
  transfers between devices with their start and end apart: 5, of which 2 were waited for; matrix products, arithmetic and copies ran while one was open for 0% of the time, Pallas kernels for 9%

profile of v3, /device:TPU:1, one launch (start us, length us, event | category | flops | bytes accessed | tf_op | source)
XLA Modules:
  0.0 51.2 jit_solution(16343522936545090064)
XLA Ops:
  0.0 1.1 %select_convert_fusion = (bf16[4,16,1024]{2,1,0:T(8,128)(2,1)S(1)}, bf16[4,16,1024]{2,1,0:T(8,128)(2,1)S(1)}) fusion(s32[4,32,1024]{2,1,0:T(8,128)} %vol.1, pred[]{:T(512)S(6)} %eq.5), kind=kLoop, calls=%fused_computation | loop fusion | flops 262144 | bytes 786433 | tf_op jit(solution)/shard_map/convert_element_type | solution.py:288
  1.1 0.7 %collective-permute-start.1 = (bf16[4,16,1024]{2,1,0:T(8,128)(2,1)S(1)}, bf16[4,16,1024]{2,1,0:T(8,128)(2,1)S(1)}, u32[]{:S(2)}, u32[]{:S(2)}) collective-permute-start(bf16[4,16,1024]{2,1,0:T(8,128)(2,1)S(1)} %get-tuple-element.25), channel_id=1, source_target_pairs={{1,2},{2,1},{3,4},{4,3},{5,6},{6,5},{9,10},{10,9},{11,12},{12,11},... | collective-permute-start | bytes 393224 | tf_op jit(solution)/shard_map/ppermute | solution.py:288
  1.8 6.1 %collective-permute-start = (bf16[4,16,1024]{2,1,0:T(8,128)(2,1)S(1)}, bf16[4,16,1024]{2,1,0:T(8,128)(2,1)S(1)}, u32[]{:S(2)}, u32[]{:S(2)}) collective-permute-start(bf16[4,16,1024]{2,1,0:T(8,128)(2,1)S(1)} %get-tuple-element.26), channel_id=1, source_target_pairs={{0,1},{1,0},{2,3},{3,2},{4,5},{5,4},{6,7},{7,6},{8,9},{9,8},{10,11... | collective-permute-start | bytes 393224 | tf_op jit(solution)/shard_map/ppermute | solution.py:287
  7.9 0.1 pad_add_fusion.ids
  8.0 0.0 copy-start
  8.0 1.0 %copy-done = s32[4,32,1024]{2,1,0:T(8,128)S(1)} copy-done((s32[4,32,1024]{2,1,0:T(8,128)S(1)}, s32[4,32,1024]{2,1,0:T(8,128)}, u32[]{:S(2)}) %copy-start) | copy-done | bytes 524312
  9.0 0.0 copy-start.1
  9.0 0.7 %copy-done.1 = s32[2,4]{1,0:T(2,128)S(1)} copy-done((s32[2,4]{1,0:T(2,128)S(1)}, s32[2,4]{1,0:T(2,128)}, u32[]{:S(2)}) %copy-start.1) | copy-done | bytes 56
  9.7 0.0 copy-start.2
  9.7 0.7 %copy-done.2 = s32[4,256]{1,0:T(4,128)S(1)} copy-done((s32[4,256]{1,0:T(4,128)S(1)}, s32[4,256]{1,0:T(4,128)}, u32[]{:S(2)}) %copy-start.2) | copy-done | bytes 4120
  10.4 4.7 %shard_map.37 = (bf16[2,4,128,1024]{3,2,1,0:T(8,128)(2,1)S(1)}, bf16[4,256,256]{2,1,0:T(8,128)(2,1)S(1)}, bf16[2,4,128,256]{3,2,1,0:T(8,128)(2,1)S(1)}, f32[2,32,64]{2,1,0:T(8,128)S(1)}, f32[4,256]{1,0:T(4,128)S(1)}) custom-call(s32[4]{0:T(128)S(1)} %pad_add_fusion.ids, s32[2,4]{1,0:T(2,128)S(1)} %copy-done.1, s32[4,256]{1,0:T(4,128)S(1)} %copy-done.2, ...), custom_call_target="tpu_custom_call" | custom-call | tf_op jit(solution)/shard_map/pallas_call | solution.py:259
  15.1 0.0 collective-permute-done.1.got_b
  15.1 0.0 collective-permute-done.got_a
  15.1 3.9 %shard_map.38 = (f32[16,64,128]{2,1,0:T(8,128)S(1)}, bf16[16,64,128]{2,1,0:T(8,128)(2,1)S(1)}) custom-call(s32[4]{0:T(128)S(1)} %pad_add_fusion.ids, s32[2,4]{1,0:T(2,128)S(1)} %copy-done.1, f32[4,256]{1,0:T(4,128)S(1)} %get-tuple-element.16.palette, bf16[4,256,256]{2,1,0:T(8,128)(2,1)S(1)} %get-tuple-element.17.filter_x, ...), custom_call_target="tpu_custom_call" | custom-call | tf_op jit(solution)/shard_map/pallas_call | solution.py:259
  19.0 1.3 %collective-permute-start.2 = (bf16[16,64,128]{2,1,0:T(8,128)(2,1)S(1)}, bf16[16,64,128]{2,1,0:T(8,128)(2,1)S(1)}, u32[]{:S(2)}, u32[]{:S(2)}) collective-permute-start(bf16[16,64,128]{2,1,0:T(8,128)(2,1)S(1)} %get-tuple-element.21), channel_id=1, source_target_pairs={{0,8},{8,0},{16,24},{24,16},{32,40},{40,32},{48,56},{56,48},{64,72... | collective-permute-start | bytes 786440 | tf_op jit(solution)/shard_map/ppermute | solution.py:309
  20.4 1.2 %collective-permute-done.2.got = bf16[16,64,128]{2,1,0:T(8,128)(2,1)S(1)} collective-permute-done((bf16[16,64,128]{2,1,0:T(8,128)(2,1)S(1)}, bf16[16,64,128]{2,1,0:T(8,128)(2,1)S(1)}, u32[]{:S(2)}, u32[]{:S(2)}) %collective-permute-start.2) | collective-permute-done | bytes 262176 | tf_op jit(solution)/shard_map/ppermute | solution.py:309
  21.5 0.8 %shard_map.39 = bf16[16,64,128]{2,1,0:T(8,128)(2,1)S(1)} custom-call(s32[4]{0:T(128)S(1)} %pad_add_fusion.ids, s32[2,4]{1,0:T(2,128)S(1)} %copy-done.1, f32[16,64,128]{2,1,0:T(8,128)S(1)} %get-tuple-element.20.keep, bf16[16,64,128]{2,1,0:T(8,128)(2,1)S(1)} %collective-permute-done.2.got), custom_call_target="tpu_custom_call" | custom-call | tf_op jit(solution)/shard_map/pallas_call | solution.py:259
  22.3 20.0 %all_to_all.5.arrived = bf16[16,64,128]{2,1,0:T(8,128)(2,1)S(1)} all-to-all(bf16[16,64,128]{2,1,0:T(8,128)(2,1)S(1)} %shard_map.39), channel_id=1, replica_groups={{0,16,32,48,64,80,96,112,128,144,160,176,192,208,224,240},{8,24,40,56,7..., dimensions={0} | all-to-all | bytes 524288 | tf_op jit(solution)/shard_map/all_to_all | solution.py:311
  42.3 0.7 %shard_map.40 = (f32[2,32,128]{2,1,0:T(8,128)S(1)}, f32[2,16,128]{2,1,0:T(8,128)S(1)}, f32[2,16,128]{2,1,0:T(8,128)S(1)}) custom-call(s32[4]{0:T(128)S(1)} %pad_add_fusion.ids, s32[2,4]{1,0:T(2,128)S(1)} %copy-done.1, bf16[16,64,128]{2,1,0:T(8,128)(2,1)S(1)} %all_to_all.5.arrived), custom_call_target="tpu_custom_call" | custom-call | tf_op jit(solution)/shard_map/pallas_call | solution.py:259
  43.1 2.0 %collective-permute-start.3 = (f32[2,16,128]{2,1,0:T(8,128)S(1)}, f32[2,16,128]{2,1,0:T(8,128)S(1)}, u32[]{:S(2)}, u32[]{:S(2)}) collective-permute-start(f32[2,16,128]{2,1,0:T(8,128)S(1)} %get-tuple-element.23), channel_id=1, source_target_pairs={{0,8},{8,0},{16,24},{24,16},{32,40},{40,32},{48,56},{56,48},{64,72... | collective-permute-start | bytes 49160 | tf_op jit(solution)/shard_map/ppermute | solution.py:322
  45.1 2.0 %collective-permute-start.4 = (f32[2,16,128]{2,1,0:T(8,128)S(1)}, f32[2,16,128]{2,1,0:T(8,128)S(1)}, u32[]{:S(2)}, u32[]{:S(2)}) collective-permute-start(f32[2,16,128]{2,1,0:T(8,128)S(1)} %get-tuple-element.24), channel_id=1, source_target_pairs={{8,16},{16,8},{24,32},{32,24},{40,48},{48,40},{56,64},{64,56},{72,... | collective-permute-start | bytes 49160 | tf_op jit(solution)/shard_map/ppermute | solution.py:323
  47.1 0.0 collective-permute-done.3.got_a
  47.1 3.0 %collective-permute-done.4.got_b = f32[2,16,128]{2,1,0:T(8,128)S(1)} collective-permute-done((f32[2,16,128]{2,1,0:T(8,128)S(1)}, f32[2,16,128]{2,1,0:T(8,128)S(1)}, u32[]{:S(2)}, u32[]{:S(2)}) %collective-permute-start.4) | collective-permute-done | bytes 16416 | tf_op jit(solution)/shard_map/ppermute | solution.py:323
  50.1 1.1 %shard_map.41 = f32[2,32,4,32]{3,2,1,0:T(4,128)} custom-call(f32[2,32,64]{2,1,0:T(8,128)S(1)} %get-tuple-element.15.filter_w, f32[2,32,128]{2,1,0:T(8,128)S(1)} %get-tuple-element.22.strip_in, f32[2,16,128]{2,1,0:T(8,128)S(1)} %collective-permute-done.3.got_a, f32[2,16,128]{2,1,0:T(8,128)S(1)} %collective-permute-done.4.got_b), custom_call_target="tpu_custom_call" | custom-call | tf_op jit(solution)/shard_map/pallas_call | solution.py:259
Async XLA Ops:
  1.1 14.0 %collective-permute-start.1 = (bf16[4,16,1024]{2,1,0:T(8,128)(2,1)S(1)}, bf16[4,16,1024]{2,1,0:T(8,128)(2,1)S(1)}, u32[]{:S(2)}, u32[]{:S(2)}) collective-permute-start(bf16[4,16,1024]{2,1,0:T(8,128)(2,1)S(1)} %get-tuple-element.25), channel_id=1, source_target_pairs={{1,2},{2,1},{3,4},{4,3},{5,6},{6,5},{9,10},{10,9},{11,12},{12,11},... | collective-permute-start | bytes 393224 | tf_op jit(solution)/shard_map/ppermute | solution.py:288
  1.8 13.3 %collective-permute-start = (bf16[4,16,1024]{2,1,0:T(8,128)(2,1)S(1)}, bf16[4,16,1024]{2,1,0:T(8,128)(2,1)S(1)}, u32[]{:S(2)}, u32[]{:S(2)}) collective-permute-start(bf16[4,16,1024]{2,1,0:T(8,128)(2,1)S(1)} %get-tuple-element.26), channel_id=1, source_target_pairs={{0,1},{1,0},{2,3},{3,2},{4,5},{5,4},{6,7},{7,6},{8,9},{9,8},{10,11... | collective-permute-start | bytes 393224 | tf_op jit(solution)/shard_map/ppermute | solution.py:287
  8.0 1.0 %copy-start = (s32[4,32,1024]{2,1,0:T(8,128)S(1)}, s32[4,32,1024]{2,1,0:T(8,128)}, u32[]{:S(2)}) copy-start(s32[4,32,1024]{2,1,0:T(8,128)} %vol.1) | copy-start | bytes 1572868
  9.0 0.7 %copy-start.1 = (s32[2,4]{1,0:T(2,128)S(1)}, s32[2,4]{1,0:T(2,128)}, u32[]{:S(2)}) copy-start(s32[2,4]{1,0:T(2,128)} %view.7) | copy-start | bytes 100
  9.7 0.7 %copy-start.2 = (s32[4,256]{1,0:T(4,128)S(1)}, s32[4,256]{1,0:T(4,128)}, u32[]{:S(2)}) copy-start(s32[4,256]{1,0:T(4,128)} %tf.1) | copy-start | bytes 12292
  19.0 2.5 %collective-permute-start.2 = (bf16[16,64,128]{2,1,0:T(8,128)(2,1)S(1)}, bf16[16,64,128]{2,1,0:T(8,128)(2,1)S(1)}, u32[]{:S(2)}, u32[]{:S(2)}) collective-permute-start(bf16[16,64,128]{2,1,0:T(8,128)(2,1)S(1)} %get-tuple-element.21), channel_id=1, source_target_pairs={{0,8},{8,0},{16,24},{24,16},{32,40},{40,32},{48,56},{56,48},{64,72... | collective-permute-start | bytes 786440 | tf_op jit(solution)/shard_map/ppermute | solution.py:309
  43.1 4.0 %collective-permute-start.3 = (f32[2,16,128]{2,1,0:T(8,128)S(1)}, f32[2,16,128]{2,1,0:T(8,128)S(1)}, u32[]{:S(2)}, u32[]{:S(2)}) collective-permute-start(f32[2,16,128]{2,1,0:T(8,128)S(1)} %get-tuple-element.23), channel_id=1, source_target_pairs={{0,8},{8,0},{16,24},{24,16},{32,40},{40,32},{48,56},{56,48},{64,72... | collective-permute-start | bytes 49160 | tf_op jit(solution)/shard_map/ppermute | solution.py:322
  45.1 5.0 %collective-permute-start.4 = (f32[2,16,128]{2,1,0:T(8,128)S(1)}, f32[2,16,128]{2,1,0:T(8,128)S(1)}, u32[]{:S(2)}, u32[]{:S(2)}) collective-permute-start(f32[2,16,128]{2,1,0:T(8,128)S(1)} %get-tuple-element.24), channel_id=1, source_target_pairs={{8,16},{16,8},{24,32},{32,24},{40,48},{48,40},{56,64},{64,56},{72,... | collective-permute-start | bytes 49160 | tf_op jit(solution)/shard_map/ppermute | solution.py:323

commit v4 on v3

v4 whole, which is shorter than its diff:
```python
import jax
import jax.numpy as jnp
from jax import lax
from jax.experimental import pallas as pl
from jax.experimental.pallas import tpu as pltpu
from jax.sharding import PartitionSpec as P

VIEWS = 2
HALO = 16
LANES = 128
CENTER = 64
VMEM_LIMIT = 16 * 2**20


def sinc(t):
    angle = jnp.where(t == 0.0, 1.0, jnp.pi * t)
    return jnp.where(t == 0.0, 1.0, jnp.sin(angle) / angle)


def lanczos(offset):
    return jnp.where(jnp.abs(offset) < 3.0, sinc(offset) * sinc(offset / 3.0), 0.0)


def iota(shape, dim):
    return lax.broadcasted_iota(jnp.int32, shape, dim)


def pairs(size, first):
    out = []
    for a in range(first, size - 1, 2):
        out += [(a, a + 1), (a + 1, a)]
    return out


def lane_pick(row, index):
    table = jnp.broadcast_to(row, index.shape)
    return jnp.take_along_axis(table, index, axis=1, mode="promise_in_bounds")


def classify(code, palette, out, k, last, group):
    high = code >= LANES
    low = code & (LANES - 1)
    for c in range(4):
        value = jnp.where(
            high,
            lane_pick(palette[c : c + 1, LANES:], low),
            lane_pick(palette[c : c + 1, :LANES], low),
        )
        if k == 0:
            value = jnp.where(iota(value.shape, 1) >= CENTER, value, 0.0)
        if k == last:
            value = jnp.where(iota(value.shape, 1) < CENTER, value, 0.0)
        out[c * group : (c + 1) * group, k * LANES : (k + 1) * LANES] = value.astype(jnp.bfloat16)


def shear_columns(voxels, palette, weights, classed, store):
    group, width = voxels.shape
    blocks = width // LANES
    side = jnp.zeros((group, CENTER), jnp.int32)
    voxels = jnp.concatenate([side, voxels, side], axis=1)
    for k in range(blocks + 1):
        classify(voxels[:, k * LANES : (k + 1) * LANES], palette, classed, k, blocks, group)
    for k in range(blocks):
        part = jnp.dot(
            classed[:, k * LANES : (k + 2) * LANES], weights, preferred_element_type=jnp.float32
        ).astype(jnp.bfloat16)
        for v in range(VIEWS):
            store(v, k, part[:, v * LANES : (v + 1) * LANES])


def own_kernel(
    scalars, tables, vol, params, palette_out, own, filter_x, filter_y, filter_w, classed
):
    slab, rows, width = vol.shape
    for i in range(1 + VIEWS):
        for j in range(4):
            params[i, j] = scalars[4 + i, j]
    depth_rank, band_rank = scalars[4, 0], scalars[4, 1]
    depth = slab * scalars[4, 2]
    height = rows * scalars[4, 3]
    strip = filter_w.shape[1]

    codes = tables[0:4].astype(jnp.float32)
    opacity = codes[3:4] / (64.0 * depth.astype(jnp.float32))
    premult = codes[0:3] / 255.0 * opacity
    palette = jnp.concatenate([premult, opacity], axis=0).astype(jnp.bfloat16).astype(jnp.float32)
    palette_out[...] = palette

    which = iota((VIEWS * slab, LANES), 0)
    lane = iota((VIEWS * slab, LANES), 1)
    place = depth_rank * slab + which % slab
    taps = []
    for column in range(2):
        q = jnp.where(which < slab, scalars[5, column], scalars[6, column])
        num = q * (2 * place + 1 - depth)
        whole = num // (2 * depth)
        frac = (num - whole * (2 * depth)).astype(jnp.float32) / (2.0 * depth.astype(jnp.float32))
        taps.append(
            lanczos(frac - (lane - CENTER).astype(jnp.float32))
            .astype(jnp.bfloat16)
            .astype(jnp.float32)
        )

    def shift(v, s, column):
        num = scalars[5 + v, column] * (2 * (depth_rank * slab + s) + 1 - depth)
        return num // (2 * depth)

    base_x = iota((2 * LANES, LANES), 0) - iota((2 * LANES, LANES), 1)
    for s in range(slab):
        for v in range(VIEWS):
            row = taps[0][v * slab + s : v * slab + s + 1]
            index = jnp.clip(base_x - shift(v, s, 0), 0, LANES - 1)
            filter_x[s, :, v * LANES : (v + 1) * LANES] = lane_pick(row, index).astype(jnp.bfloat16)

        def store(v, k, part):
            own[v, s, :, k * LANES : (k + 1) * LANES] = part

        shear_columns(vol[s].astype(jnp.int32), palette, filter_x[s], classed, store)

    lanes = 4 * rows
    to = iota((lanes, lanes), 0)
    frm = iota((lanes, lanes), 1)
    even = band_rank % 2 == 0
    start_a = jnp.where(even, rows, -HALO)
    start_b = jnp.where(even, -HALO, rows)
    at = frm % rows
    base_y = []
    for local in (at, jnp.where(at < HALO, at + start_a, at - HALO + start_b)):
        world = local + band_rank * rows
        fits = (to // rows == frm // rows) & (world >= 0) & (world < height)
        base_y.append(jnp.where(fits, local - to % rows + CENTER, -4 * LANES))
    for v in range(VIEWS):
        for s in range(slab):
            row = taps[1][v * slab + s : v * slab + s + 1]
            for j in range(2):
                index = jnp.clip(base_y[j] - shift(v, s, 1), 0, LANES - 1)
                filter_y[v, s, :, j * lanes : (j + 1) * lanes] = lane_pick(row, index).astype(
                    jnp.bfloat16
                )

    shape = (strip, strip + 2 * HALO)
    local = iota(shape, 1) - HALO
    column = iota(shape, 0)
    for v in range(VIEWS):
        num = scalars[5 + v, 2] * (2 * (depth_rank * strip + column) + 1 - width) + width
        whole = num // (2 * width)
        frac = (num - whole * (2 * width)).astype(jnp.float32) / (2.0 * width)
        filter_w[v] = lanczos(frac - (local - column - whole).astype(jnp.float32))


def slab_kernel(
    params, palette, filter_x, filter_y, own, got_a, got_b, keep, send, classed, near
):
    slab = own.shape[1]
    lanes, width = own.shape[2:]
    rows = lanes // 4
    for s in range(slab):

        def store(v, k, part):
            near[v, s, :, k * LANES : (k + 1) * LANES] = part

        voxels = jnp.concatenate(
            [got_a[s].astype(jnp.int32), got_b[s].astype(jnp.int32)], axis=0
        )
        shear_columns(voxels, palette[...], filter_x[s], classed, store)
    chunk = 2 * LANES
    for v in range(VIEWS):
        facing = params[1 + v, 3] >= 0
        for side in (slice(0, HALO), slice(HALO + width, 2 * HALO + width)):
            keep[v, side] = jnp.zeros((HALO, lanes), jnp.float32)
            send[v, side] = jnp.zeros((HALO, lanes), jnp.bfloat16)
        for k in range(width // chunk):
            for step in range(slab):
                s = jnp.where(facing, step, slab - 1 - step)
                source = jnp.concatenate(
                    [
                        own[v, s, :, k * chunk : (k + 1) * chunk],
                        near[v, s, :, k * chunk : (k + 1) * chunk],
                    ],
                    axis=0,
                )
                sheared = jnp.dot(filter_y[v, s], source, preferred_element_type=jnp.float32)
                if step == 0:
                    picture = sheared
                    continue
                through = 1.0 - picture[3 * rows :]
                picture = picture + jnp.concatenate([through] * 4, axis=0) * sheared
            turned = picture.T
            at = slice(HALO + k * chunk, HALO + (k + 1) * chunk)
            keep[v, at] = turned
            send[v, at] = turned.astype(jnp.bfloat16)


def merge_kernel(params, keep, got, out):
    strips, both, lanes = out.shape
    span = both // VIEWS
    rows = lanes // 4
    core = params[0, 0] % 2
    pick = 3 * rows + iota((span, lanes), 1) % rows
    for v in range(VIEWS):
        mine_front = (params[1 + v, 3] >= 0) == (core == 0)
        for k in range(strips):
            at = pl.ds(pl.multiple_of(k * span + core * (span // 2), span // 2), span)
            mine = keep[v, at]
            other = got[v, at].astype(jnp.float32)
            front = jnp.where(mine_front, mine, other)
            back = jnp.where(mine_front, other, mine)
            alpha = jnp.take_along_axis(front, pick, axis=1, mode="promise_in_bounds")
            out[k, v * span : (v + 1) * span] = (front + (1.0 - alpha) * back).astype(
                jnp.bfloat16
            )


def final_kernel(params, filter_w, arrived, out):
    slabs, both, lanes = arrived.shape
    span = both // VIEWS
    rows = lanes // 4
    pick = 3 * rows + iota((span, lanes), 1) % rows
    for v in range(VIEWS):
        facing = params[1 + v, 3] >= 0
        picture = jnp.zeros((span, lanes), jnp.float32)
        through = jnp.ones((span, lanes), jnp.float32)
        for k in range(slabs):
            at = jnp.where(facing, k, slabs - 1 - k)
            part = arrived[at, v * span : (v + 1) * span, :].astype(jnp.float32)
            picture = picture + through * part
            through = through * (
                1.0 - jnp.take_along_axis(part, pick, axis=1, mode="promise_in_bounds")
            )
        final = jnp.dot(
            filter_w[v],
            picture,
            precision=lax.Precision.HIGHEST,
            preferred_element_type=jnp.float32,
        )
        for c in range(4):
            out[v, :, c, :] = final[:, c * rows : (c + 1) * rows]


def call(kernel, outs, scratch=(), spaces=(), out_spaces=None):
    def run(*args):
        given = list(spaces) + [pltpu.VMEM] * (len(args) - len(spaces))
        where = out_spaces or jax.tree.map(lambda _: pltpu.VMEM, outs)
        return pl.pallas_call(
            kernel,
            out_shape=outs,
            in_specs=[pl.BlockSpec(memory_space=space) for space in given],
            out_specs=jax.tree.map(lambda space: pl.BlockSpec(memory_space=space), where),
            scratch_shapes=list(scratch),
            compiler_params=pltpu.CompilerParams(vmem_limit_bytes=VMEM_LIMIT),
        )(*args)

    return run


def body(volume, tf_table, view_code):
    slab, rows, width = volume.shape
    depth_size = lax.axis_size("depth")
    band_size = lax.axis_size("band")
    strip = width // depth_size
    lanes = 4 * rows
    bf16, f32, i32 = jnp.bfloat16, jnp.float32, jnp.int32
    shape = jax.ShapeDtypeStruct
    smem = (pltpu.SMEM,)
    ids = jnp.stack(
        [lax.axis_index("depth"), lax.axis_index("band"), jnp.int32(depth_size), jnp.int32(band_size)]
    ).astype(i32)
    wide = tf_table.shape[1]
    tables = jnp.concatenate(
        [tf_table]
        + [jnp.pad(part, ((0, 0), (0, wide - 4))) for part in (ids[None], view_code)]
        + [jnp.zeros((1, wide), i32)],
        axis=0,
    )
    voxels = volume.astype(bf16)
    even = lax.axis_index("band") % 2 == 0
    first = voxels[:, :HALO]
    last = voxels[:, rows - HALO :]
    send_a = jnp.where(even, last, first)
    send_b = jnp.where(even, first, last)
    got_a = lax.ppermute(send_a, "band", pairs(band_size, 0))
    got_b = lax.ppermute(send_b, "band", pairs(band_size, 1))
    params, palette, own, filter_x, filter_y, filter_w = call(
        own_kernel,
        (
            shape((1 + VIEWS, 4), i32),
            shape(tf_table.shape, f32),
            shape((VIEWS, slab, lanes, width), bf16),
            shape((slab, 2 * LANES, VIEWS * LANES), bf16),
            shape((VIEWS, slab, lanes, 2 * lanes), bf16),
            shape((VIEWS, strip, strip + 2 * HALO), f32),
        ),
        (pltpu.VMEM((lanes, width + LANES), bf16),),
        smem,
        (pltpu.SMEM,) + (pltpu.VMEM,) * 5,
    )(tables, tables, voxels)
    padded = (VIEWS, width + 2 * HALO, lanes)
    keep, send = call(
        slab_kernel,
        (shape(padded, f32), shape(padded, bf16)),
        (
            pltpu.VMEM((8 * HALO, width + LANES), bf16),
            pltpu.VMEM((VIEWS, slab, 8 * HALO, width), bf16),
        ),
        smem,
    )(params, palette, filter_x, filter_y, own, got_a, got_b)
    got = lax.ppermute(send, "depth", pairs(depth_size, 0))
    merged = shape((depth_size // 2, VIEWS * (strip + 2 * HALO), lanes), bf16)
    merged = call(merge_kernel, merged, (), smem)(params, keep, got)
    arrived = lax.all_to_all(
        merged,
        "depth",
        split_axis=0,
        concat_axis=0,
        tiled=True,
        axis_index_groups=[list(range(i, depth_size, 2)) for i in range(2)],
    )
    final = shape((VIEWS, strip, 4, rows), f32)
    return call(final_kernel, final, (), smem)(params, filter_w, arrived)


def solution(mesh):
    placed = (P("depth", "band", None), P(), P())
    return jax.shard_map(
        body, mesh=mesh, in_specs=placed, out_specs=P(None, "depth", None, "band"), check_vma=False
    )
```

time: 51.5 us -> 50.2 us (0.975)
  the two profiles are of different devices: /device:TPU:1 before, /device:TPU:16 now
where the time goes in v4:
time: 50.2 us; the launch traced here: 49.7 us
  blocking collectives  27.3 us (54%)
  Pallas kernels  12.1 us (24%)
  starting transfers between devices  6.34 us (13%)
  other arithmetic  1.95 us (4%)
  waiting for transfers between devices  1.93 us (4%)
    all_to_all x1, blocking collectives, body(): lax.all_to_all(merged, 'depth', split_axis=0, concat_axis=0, tiled=True,...  27.3 us
    pallas_call x4, Pallas kernels, run(): pl.pallas_call(kernel, out_shape=outs, in_specs=[pl.BlockSpec(memory_spac...  12.1 us
    ppermute x1, starting transfers between devices, body(): got_b = lax.ppermute(send_b, 'band', pairs(band_size, 1))  4.82 us
    ppermute x1, waiting for transfers between devices, body(): got = lax.ppermute(send, 'depth', pairs(depth_size, 0))  1.92 us
    ppermute x1, starting transfers between devices, body(): got_a = lax.ppermute(send_a, 'band', pairs(band_size, 0))  1.43 us
    convert_element_type x1, other arithmetic, body(): voxels = volume.astype(bf16)  1.07 us
  transfers between devices with their start and end apart: 3, of which 1 were waited for; matrix products, arithmetic and copies ran while one was open for 2% of the time, Pallas kernels for 11%

profile of v4, /device:TPU:16, one launch (start us, length us, event | category | flops | bytes accessed | tf_op | source)
XLA Modules:
  0.0 49.7 jit_solution(14399011128065121271)
XLA Ops:
  0.0 1.1 %convert_element_type.3.vol = bf16[4,32,1024]{2,1,0:T(8,128)(2,1)S(1)} convert(s32[4,32,1024]{2,1,0:T(8,128)} %param.3) | non-fusion elementwise | flops 131072 | bytes 786432 | tf_op jit(solution)/shard_map/convert_element_type | solution.py:275
  1.1 4.8 %collective-permute-start.1 = (bf16[4,16,1024]{2,1,0:T(8,128)(2,1)S(1)}, bf16[4,16,1024]{2,1,0:T(8,128)(2,1)S(1)}, u32[]{:S(2)}, u32[]{:S(2)}) collective-permute-start(bf16[4,16,1024]{2,1,0:T(8,128)(2,1)S(1)} %get-tuple-element.21), channel_id=1, source_target_pairs={{1,2},{2,1},{3,4},{4,3},{5,6},{6,5},{9,10},{10,9},{11,12},{12,11},... | collective-permute-start | bytes 393224 | tf_op jit(solution)/shard_map/ppermute | solution.py:282
  5.9 1.4 %collective-permute-start = (bf16[4,16,1024]{2,1,0:T(8,128)(2,1)S(1)}, bf16[4,16,1024]{2,1,0:T(8,128)(2,1)S(1)}, u32[]{:S(2)}, u32[]{:S(2)}) collective-permute-start(bf16[4,16,1024]{2,1,0:T(8,128)(2,1)S(1)} %get-tuple-element.22), channel_id=1, source_target_pairs={{0,1},{1,0},{2,3},{3,2},{4,5},{5,4},{6,7},{7,6},{8,9},{9,8},{10,11... | collective-permute-start | bytes 393224 | tf_op jit(solution)/shard_map/ppermute | solution.py:281
  7.4 0.1 pad.13.clone
  7.4 0.1 add_bitcast_fusion
  7.5 0.8 %fusion.scalars.tables = s32[8,256]{1,0:T(8,128)S(1)} fusion(s32[2,4]{1,0:T(2,128)} %param.5, s32[1,4]{1,0:T(1,128)S(1)} %add_bitcast_fusion, s32[4,256]{1,0:T(4,128)} %param.4, s32[8]{0:T(128)S(1)} %pad.13.clone), kind=kLoop, calls=%fused_computation.3 | loop fusion | flops 6144 | bytes 12368 | tf_op jit(solution)/shard_map/concatenate | solution.py:269
  8.3 5.2 %shard_map.37 = (s32[3,4]{1,0:T(4,128)S(1)}, f32[4,256]{1,0:T(4,128)S(1)}, bf16[2,4,128,1024]{3,2,1,0:T(8,128)(2,1)S(1)}, bf16[4,256,256]{2,1,0:T(8,128)(2,1)S(1...) custom-call(s32[8,256]{1,0:T(8,128)S(1)} %fusion.scalars.tables, s32[8,256]{1,0:T(8,128)S(1)} %fusion.scalars.tables, ...), custom_call_target="tpu_custom_call" | custom-call | tf_op jit(solution)/shard_map/pallas_call | solution.py:244
  13.5 0.0 collective-permute-done.1.got_b
  13.6 0.0 collective-permute-done.got_a
  13.6 3.9 %shard_map.38 = (f32[2,1056,128]{2,1,0:T(8,128)S(1)}, bf16[2,1056,128]{2,1,0:T(8,128)(2,1)S(1)}) custom-call(s32[3,4]{1,0:T(4,128)S(1)} %get-tuple-element.13.params, f32[4,256]{1,0:T(4,128)S(1)} %get-tuple-element.15.palette, bf16[4,256,256]{2,1,0:T(8,128)(2,1)S(1)} %get-tuple-element.16.filter_x, bf16[2,4,128,256]{3,2,1,0:T(8,128)(2,1)S(1)} %get-tuple-element.17.filter_y, ...), custom_call_target="tpu_custom_call" | custom-call | tf_op jit(solution)/shard_map/pallas_call | solution.py:244
  17.5 0.1 collective-permute-start.2
  17.6 1.9 %collective-permute-done.2.got = bf16[2,1056,128]{2,1,0:T(8,128)(2,1)S(1)} collective-permute-done((bf16[2,1056,128]{2,1,0:T(8,128)(2,1)S(1)}, bf16[2,1056,128]{2,1,0:T(8,128)(2,1)S(1)}, u32[]{:S(2)}, u32[]{:S(2)}) %collective-permute-start.2) | collective-permute-done | bytes 540704 | tf_op jit(solution)/shard_map/ppermute | solution.py:307
  19.5 0.9 %shard_map.39 = bf16[16,128,128]{2,1,0:T(8,128)(2,1)S(1)} custom-call(s32[3,4]{1,0:T(4,128)S(1)} %get-tuple-element.13.params, f32[2,1056,128]{2,1,0:T(8,128)S(1)} %get-tuple-element.19.keep, bf16[2,1056,128]{2,1,0:T(8,128)(2,1)S(1)} %collective-permute-done.2.got), custom_call_target="tpu_custom_call" | custom-call | tf_op jit(solution)/shard_map/pallas_call | solution.py:244
  20.5 27.3 %all_to_all.5.arrived = bf16[16,128,128]{2,1,0:T(8,128)(2,1)S(1)} all-to-all(bf16[16,128,128]{2,1,0:T(8,128)(2,1)S(1)} %shard_map.39), channel_id=1, replica_groups={{0,16,32,48,64,80,96,112,128,144,160,176,192,208,224,240},{8,24,40,56,7..., dimensions={0} | all-to-all | bytes 1048576 | tf_op jit(solution)/shard_map/all_to_all | solution.py:310
  47.7 1.9 %shard_map.40 = f32[2,32,4,32]{3,2,1,0:T(4,128)} custom-call(s32[3,4]{1,0:T(4,128)S(1)} %get-tuple-element.13.params, f32[2,32,64]{2,1,0:T(8,128)S(1)} %get-tuple-element.14.filter_w, bf16[16,128,128]{2,1,0:T(8,128)(2,1)S(1)} %all_to_all.5.arrived), custom_call_target="tpu_custom_call" | custom-call | tf_op jit(solution)/shard_map/pallas_call | solution.py:244
  (1 shorter events, 0.0 us)
Async XLA Ops:
  1.1 12.4 %collective-permute-start.1 = (bf16[4,16,1024]{2,1,0:T(8,128)(2,1)S(1)}, bf16[4,16,1024]{2,1,0:T(8,128)(2,1)S(1)}, u32[]{:S(2)}, u32[]{:S(2)}) collective-permute-start(bf16[4,16,1024]{2,1,0:T(8,128)(2,1)S(1)} %get-tuple-element.21), channel_id=1, source_target_pairs={{1,2},{2,1},{3,4},{4,3},{5,6},{6,5},{9,10},{10,9},{11,12},{12,11},... | collective-permute-start | bytes 393224 | tf_op jit(solution)/shard_map/ppermute | solution.py:282
  5.9 7.6 %collective-permute-start = (bf16[4,16,1024]{2,1,0:T(8,128)(2,1)S(1)}, bf16[4,16,1024]{2,1,0:T(8,128)(2,1)S(1)}, u32[]{:S(2)}, u32[]{:S(2)}) collective-permute-start(bf16[4,16,1024]{2,1,0:T(8,128)(2,1)S(1)} %get-tuple-element.22), channel_id=1, source_target_pairs={{0,1},{1,0},{2,3},{3,2},{4,5},{5,4},{6,7},{7,6},{8,9},{9,8},{10,11... | collective-permute-start | bytes 393224 | tf_op jit(solution)/shard_map/ppermute | solution.py:281
  17.5 2.0 %collective-permute-start.2 = (bf16[2,1056,128]{2,1,0:T(8,128)(2,1)S(1)}, bf16[2,1056,128]{2,1,0:T(8,128)(2,1)S(1)}, u32[]{:S(2)}, u32[]{:S(2)}) collective-permute-start(bf16[2,1056,128]{2,1,0:T(8,128)(2,1)S(1)} %get-tuple-element.20), channel_id=1, source_target_pairs={{0,8},{8,0},{16,24},{24,16},{32,40},{40,32},{48,56},{56,48},{64,72... | collective-permute-start | bytes 1622024 | tf_op jit(solution)/shard_map/ppermute | solution.py:307

commit v5 on v4

--- a/solution.py
+++ b/solution.py
@@ -7,8 +7,10 @@
 
 VIEWS = 2
 HALO = 16
+MARGIN = 12
 LANES = 128
 CENTER = 64
+FAR = 20
 VMEM_LIMIT = 16 * 2**20
 
 
@@ -78,7 +80,7 @@
     depth_rank, band_rank = scalars[4, 0], scalars[4, 1]
     depth = slab * scalars[4, 2]
     height = rows * scalars[4, 3]
-    strip = filter_w.shape[1]
+    strip = filter_w.shape[0]
 
     codes = tables[0:4].astype(jnp.float32)
     opacity = codes[3:4] / (64.0 * depth.astype(jnp.float32))
@@ -106,10 +108,11 @@
         return num // (2 * depth)
 
     base_x = iota((2 * LANES, LANES), 0) - iota((2 * LANES, LANES), 1)
+    base_x = jnp.clip(base_x, FAR, LANES - 1 - FAR)
     for s in range(slab):
         for v in range(VIEWS):
             row = taps[0][v * slab + s : v * slab + s + 1]
-            index = jnp.clip(base_x - shift(v, s, 0), 0, LANES - 1)
+            index = base_x - shift(v, s, 0)
             filter_x[s, :, v * LANES : (v + 1) * LANES] = lane_pick(row, index).astype(jnp.bfloat16)
 
         def store(v, k, part):
@@ -128,24 +131,25 @@
     for local in (at, jnp.where(at < HALO, at + start_a, at - HALO + start_b)):
         world = local + band_rank * rows
         fits = (to // rows == frm // rows) & (world >= 0) & (world < height)
-        base_y.append(jnp.where(fits, local - to % rows + CENTER, -4 * LANES))
+        base_y.append(jnp.where(fits, local - to % rows + CENTER, FAR))
     for v in range(VIEWS):
         for s in range(slab):
             row = taps[1][v * slab + s : v * slab + s + 1]
             for j in range(2):
-                index = jnp.clip(base_y[j] - shift(v, s, 1), 0, LANES - 1)
+                index = base_y[j] - shift(v, s, 1)
                 filter_y[v, s, :, j * lanes : (j + 1) * lanes] = lane_pick(row, index).astype(
                     jnp.bfloat16
                 )
 
-    shape = (strip, strip + 2 * HALO)
-    local = iota(shape, 1) - HALO
+    shape = filter_w.shape
+    half = shape[1] // VIEWS
     column = iota(shape, 0)
-    for v in range(VIEWS):
-        num = scalars[5 + v, 2] * (2 * (depth_rank * strip + column) + 1 - width) + width
-        whole = num // (2 * width)
-        frac = (num - whole * (2 * width)).astype(jnp.float32) / (2.0 * width)
-        filter_w[v] = lanczos(frac - (local - column - whole).astype(jnp.float32))
+    local = iota(shape, 1) % half - MARGIN
+    q = jnp.where(iota(shape, 1) < half, scalars[5, 2], scalars[6, 2])
+    num = q * (2 * (depth_rank * strip + column) + 1 - width) + width
+    whole = num // (2 * width)
+    frac = (num - whole * (2 * width)).astype(jnp.float32) / (2.0 * width)
+    filter_w[...] = lanczos(frac - (local - column - whole).astype(jnp.float32))
 
 
 def slab_kernel(
@@ -194,21 +198,23 @@
 def merge_kernel(params, keep, got, out):
     strips, both, lanes = out.shape
     span = both // VIEWS
+    wide = span + 2 * (HALO - MARGIN)
     rows = lanes // 4
     core = params[0, 0] % 2
-    pick = 3 * rows + iota((span, lanes), 1) % rows
-    for v in range(VIEWS):
-        mine_front = (params[1 + v, 3] >= 0) == (core == 0)
-        for k in range(strips):
-            at = pl.ds(pl.multiple_of(k * span + core * (span // 2), span // 2), span)
+    pick = 3 * rows + iota((wide, lanes), 1) % rows
+    for k in range(strips):
+        at = pl.ds(pl.multiple_of(k * wide + core * (wide // 2), wide // 2), wide)
+        done = []
+        for v in range(VIEWS):
+            mine_front = (params[1 + v, 3] >= 0) == (core == 0)
             mine = keep[v, at]
             other = got[v, at].astype(jnp.float32)
             front = jnp.where(mine_front, mine, other)
             back = jnp.where(mine_front, other, mine)
             alpha = jnp.take_along_axis(front, pick, axis=1, mode="promise_in_bounds")
-            out[k, v * span : (v + 1) * span] = (front + (1.0 - alpha) * back).astype(
-                jnp.bfloat16
-            )
+            merged = front + (1.0 - alpha) * back
+            done.append(merged[HALO - MARGIN : HALO - MARGIN + span])
+        out[k] = jnp.concatenate(done, axis=0).astype(jnp.bfloat16)
 
 
 def final_kernel(params, filter_w, arrived, out):
@@ -222,13 +228,14 @@
         through = jnp.ones((span, lanes), jnp.float32)
         for k in range(slabs):
             at = jnp.where(facing, k, slabs - 1 - k)
-            part = arrived[at, v * span : (v + 1) * span, :].astype(jnp.float32)
+            part = arrived[at].astype(jnp.float32)[v * span : (v + 1) * span]
             picture = picture + through * part
             through = through * (
                 1.0 - jnp.take_along_axis(part, pick, axis=1, mode="promise_in_bounds")
             )
+        half = filter_w.shape[1] // VIEWS
         final = jnp.dot(
-            filter_w[v],
+            filter_w[:, v * half : v * half + span],
             picture,
             precision=lax.Precision.HIGHEST,
             preferred_element_type=jnp.float32,
@@ -288,7 +295,7 @@
             shape((VIEWS, slab, lanes, width), bf16),
             shape((slab, 2 * LANES, VIEWS * LANES), bf16),
             shape((VIEWS, slab, lanes, 2 * lanes), bf16),
-            shape((VIEWS, strip, strip + 2 * HALO), f32),
+            shape((strip, VIEWS * (strip + 2 * HALO)), f32),
         ),
         (pltpu.VMEM((lanes, width + LANES), bf16),),
         smem,
@@ -305,7 +312,7 @@
         smem,
     )(params, palette, filter_x, filter_y, own, got_a, got_b)
     got = lax.ppermute(send, "depth", pairs(depth_size, 0))
-    merged = shape((depth_size // 2, VIEWS * (strip + 2 * HALO), lanes), bf16)
+    merged = shape((depth_size // 2, VIEWS * (strip + 2 * MARGIN), lanes), bf16)
     merged = call(merge_kernel, merged, (), smem)(params, keep, got)
     arrived = lax.all_to_all(
         merged,

time: 50.2 us -> 48.5 us (0.966)
  blocking collectives: 27.3 us -> 25.9 us
    all_to_all x1, blocking collectives: 27.3 us -> 25.9 us  [body(): lax.all_to_all(merged, 'depth', split_axis=0, concat_axis=0, tiled=True,...]
  transfers between devices with their start and end apart: 3 -> 3, of which waited for: 1 -> 2; matrix products, arithmetic and copies ran while one was open for 2% -> 2% of each run, Pallas kernels for 11% -> 10%
where the time goes in v5:
time: 48.5 us; the launch traced here: 48 us
  blocking collectives  25.9 us (53%)
  Pallas kernels  11.7 us (24%)
  starting transfers between devices  6.34 us (13%)
  waiting for transfers between devices  2.01 us (4%)
  other arithmetic  1.95 us (4%)
    all_to_all x1, blocking collectives, body(): lax.all_to_all(merged, 'depth', split_axis=0, concat_axis=0, tiled=True,...  25.9 us
    pallas_call x4, Pallas kernels, run(): pl.pallas_call(kernel, out_shape=outs, in_specs=[pl.BlockSpec(memory_spac...  11.7 us
    ppermute x1, starting transfers between devices, body(): got_b = lax.ppermute(send_b, 'band', pairs(band_size, 1))  4.82 us
    ppermute x1, waiting for transfers between devices, body(): got = lax.ppermute(send, 'depth', pairs(depth_size, 0))  1.92 us
    ppermute x1, starting transfers between devices, body(): got_a = lax.ppermute(send_a, 'band', pairs(band_size, 0))  1.43 us
    convert_element_type x1, other arithmetic, body(): voxels = volume.astype(bf16)  1.07 us
  transfers between devices with their start and end apart: 3, of which 2 were waited for; matrix products, arithmetic and copies ran while one was open for 2% of the time, Pallas kernels for 10%

profile of v5, /device:TPU:16, one launch (start us, length us, event | category | flops | bytes accessed | tf_op | source)
XLA Modules:
  0.0 48.0 jit_solution(683506291174121323)
XLA Ops:
  0.0 1.1 %convert_element_type.3.vol = bf16[4,32,1024]{2,1,0:T(8,128)(2,1)S(1)} convert(s32[4,32,1024]{2,1,0:T(8,128)} %param.3) | non-fusion elementwise | flops 131072 | bytes 786432 | tf_op jit(solution)/shard_map/convert_element_type | solution.py:282
  1.1 4.8 %collective-permute-start.1 = (bf16[4,16,1024]{2,1,0:T(8,128)(2,1)S(1)}, bf16[4,16,1024]{2,1,0:T(8,128)(2,1)S(1)}, u32[]{:S(2)}, u32[]{:S(2)}) collective-permute-start(bf16[4,16,1024]{2,1,0:T(8,128)(2,1)S(1)} %get-tuple-element.21), channel_id=1, source_target_pairs={{1,2},{2,1},{3,4},{4,3},{5,6},{6,5},{9,10},{10,9},{11,12},{12,11},... | collective-permute-start | bytes 393224 | tf_op jit(solution)/shard_map/ppermute | solution.py:289
  5.9 1.4 %collective-permute-start = (bf16[4,16,1024]{2,1,0:T(8,128)(2,1)S(1)}, bf16[4,16,1024]{2,1,0:T(8,128)(2,1)S(1)}, u32[]{:S(2)}, u32[]{:S(2)}) collective-permute-start(bf16[4,16,1024]{2,1,0:T(8,128)(2,1)S(1)} %get-tuple-element.22), channel_id=1, source_target_pairs={{0,1},{1,0},{2,3},{3,2},{4,5},{5,4},{6,7},{7,6},{8,9},{9,8},{10,11... | collective-permute-start | bytes 393224 | tf_op jit(solution)/shard_map/ppermute | solution.py:288
  7.4 0.1 pad.13.clone
  7.4 0.1 add_bitcast_fusion
  7.5 0.8 %fusion.scalars.tables = s32[8,256]{1,0:T(8,128)S(1)} fusion(s32[2,4]{1,0:T(2,128)} %param.5, s32[1,4]{1,0:T(1,128)S(1)} %add_bitcast_fusion, s32[4,256]{1,0:T(4,128)} %param.4, s32[8]{0:T(128)S(1)} %pad.13.clone), kind=kLoop, calls=%fused_computation.3 | loop fusion | flops 6144 | bytes 12368 | tf_op jit(solution)/shard_map/concatenate | solution.py:276
  8.3 4.9 %shard_map.37 = (s32[3,4]{1,0:T(4,128)S(1)}, f32[4,256]{1,0:T(4,128)S(1)}, bf16[2,4,128,1024]{3,2,1,0:T(8,128)(2,1)S(1)}, bf16[4,256,256]{2,1,0:T(8,128)(2,1)S(1...) custom-call(s32[8,256]{1,0:T(8,128)S(1)} %fusion.scalars.tables, s32[8,256]{1,0:T(8,128)S(1)} %fusion.scalars.tables, ...), custom_call_target="tpu_custom_call" | custom-call | tf_op jit(solution)/shard_map/pallas_call | solution.py:251
  13.2 0.0 collective-permute-done.1.got_b
  13.2 0.1 collective-permute-done.got_a
  13.3 3.9 %shard_map.38 = (f32[2,1056,128]{2,1,0:T(8,128)S(1)}, bf16[2,1056,128]{2,1,0:T(8,128)(2,1)S(1)}) custom-call(s32[3,4]{1,0:T(4,128)S(1)} %get-tuple-element.13.params, f32[4,256]{1,0:T(4,128)S(1)} %get-tuple-element.15.palette, bf16[4,256,256]{2,1,0:T(8,128)(2,1)S(1)} %get-tuple-element.16.filter_x, bf16[2,4,128,256]{3,2,1,0:T(8,128)(2,1)S(1)} %get-tuple-element.17.filter_y, ...), custom_call_target="tpu_custom_call" | custom-call | tf_op jit(solution)/shard_map/pallas_call | solution.py:251
  17.2 0.1 collective-permute-start.2
  17.3 1.9 %collective-permute-done.2.got = bf16[2,1056,128]{2,1,0:T(8,128)(2,1)S(1)} collective-permute-done((bf16[2,1056,128]{2,1,0:T(8,128)(2,1)S(1)}, bf16[2,1056,128]{2,1,0:T(8,128)(2,1)S(1)}, u32[]{:S(2)}, u32[]{:S(2)}) %collective-permute-start.2) | collective-permute-done | bytes 540704 | tf_op jit(solution)/shard_map/ppermute | solution.py:314
  19.2 1.0 %shard_map.39 = bf16[16,112,128]{2,1,0:T(8,128)(2,1)S(1)} custom-call(s32[3,4]{1,0:T(4,128)S(1)} %get-tuple-element.13.params, f32[2,1056,128]{2,1,0:T(8,128)S(1)} %get-tuple-element.19.keep, bf16[2,1056,128]{2,1,0:T(8,128)(2,1)S(1)} %collective-permute-done.2.got), custom_call_target="tpu_custom_call" | custom-call | tf_op jit(solution)/shard_map/pallas_call | solution.py:251
  20.2 25.9 %all_to_all.5.arrived = bf16[16,112,128]{2,1,0:T(8,128)(2,1)S(1)} all-to-all(bf16[16,112,128]{2,1,0:T(8,128)(2,1)S(1)} %shard_map.39), channel_id=1, replica_groups={{0,16,32,48,64,80,96,112,128,144,160,176,192,208,224,240},{8,24,40,56,7..., dimensions={0} | all-to-all | bytes 917504 | tf_op jit(solution)/shard_map/all_to_all | solution.py:317
  46.1 1.9 %shard_map.40 = f32[2,32,4,32]{3,2,1,0:T(4,128)} custom-call(s32[3,4]{1,0:T(4,128)S(1)} %get-tuple-element.13.params, f32[32,128]{1,0:T(8,128)S(1)} %get-tuple-element.14.filter_w, bf16[16,112,128]{2,1,0:T(8,128)(2,1)S(1)} %all_to_all.5.arrived), custom_call_target="tpu_custom_call" | custom-call | tf_op jit(solution)/shard_map/pallas_call | solution.py:251
  (1 shorter events, 0.0 us)
Async XLA Ops:
  1.1 12.1 %collective-permute-start.1 = (bf16[4,16,1024]{2,1,0:T(8,128)(2,1)S(1)}, bf16[4,16,1024]{2,1,0:T(8,128)(2,1)S(1)}, u32[]{:S(2)}, u32[]{:S(2)}) collective-permute-start(bf16[4,16,1024]{2,1,0:T(8,128)(2,1)S(1)} %get-tuple-element.21), channel_id=1, source_target_pairs={{1,2},{2,1},{3,4},{4,3},{5,6},{6,5},{9,10},{10,9},{11,12},{12,11},... | collective-permute-start | bytes 393224 | tf_op jit(solution)/shard_map/ppermute | solution.py:289
  5.9 7.3 %collective-permute-start = (bf16[4,16,1024]{2,1,0:T(8,128)(2,1)S(1)}, bf16[4,16,1024]{2,1,0:T(8,128)(2,1)S(1)}, u32[]{:S(2)}, u32[]{:S(2)}) collective-permute-start(bf16[4,16,1024]{2,1,0:T(8,128)(2,1)S(1)} %get-tuple-element.22), channel_id=1, source_target_pairs={{0,1},{1,0},{2,3},{3,2},{4,5},{5,4},{6,7},{7,6},{8,9},{9,8},{10,11... | collective-permute-start | bytes 393224 | tf_op jit(solution)/shard_map/ppermute | solution.py:288
  17.2 2.0 %collective-permute-start.2 = (bf16[2,1056,128]{2,1,0:T(8,128)(2,1)S(1)}, bf16[2,1056,128]{2,1,0:T(8,128)(2,1)S(1)}, u32[]{:S(2)}, u32[]{:S(2)}) collective-permute-start(bf16[2,1056,128]{2,1,0:T(8,128)(2,1)S(1)} %get-tuple-element.20), channel_id=1, source_target_pairs={{0,8},{8,0},{16,24},{24,16},{32,40},{40,32},{48,56},{56,48},{64,72... | collective-permute-start | bytes 1622024 | tf_op jit(solution)/shard_map/ppermute | solution.py:314

commit v6 on v5

--- a/solution.py
+++ b/solution.py
@@ -34,14 +34,31 @@
     return out
 
 
+def lane_gather(table, index):
+    numbers = lax.GatherDimensionNumbers(
+        offset_dims=(),
+        collapsed_slice_dims=(1,),
+        start_index_map=(1,),
+        operand_batching_dims=(0,),
+        start_indices_batching_dims=(0,),
+    )
+    return lax.gather(
+        table,
+        index[..., None],
+        numbers,
+        slice_sizes=(1, 1),
+        mode=lax.GatherScatterMode.PROMISE_IN_BOUNDS,
+    )
+
+
 def lane_pick(row, index):
-    table = jnp.broadcast_to(row, index.shape)
-    return jnp.take_along_axis(table, index, axis=1, mode="promise_in_bounds")
-
-
-def classify(code, palette, out, k, last, group):
+    return lane_gather(jnp.broadcast_to(row, index.shape), index)
+
+
+def classify(code, palette, out, k, last):
     high = code >= LANES
     low = code & (LANES - 1)
+    values = []
     for c in range(4):
         value = jnp.where(
             high,
@@ -52,7 +69,8 @@
             value = jnp.where(iota(value.shape, 1) >= CENTER, value, 0.0)
         if k == last:
             value = jnp.where(iota(value.shape, 1) < CENTER, value, 0.0)
-        out[c * group : (c + 1) * group, k * LANES : (k + 1) * LANES] = value.astype(jnp.bfloat16)
+        values.append(value)
+    out[:, k * LANES : (k + 1) * LANES] = jnp.concatenate(values, axis=0).astype(jnp.bfloat16)
 
 
 def shear_columns(voxels, palette, weights, classed, store):
@@ -61,7 +79,7 @@
     side = jnp.zeros((group, CENTER), jnp.int32)
     voxels = jnp.concatenate([side, voxels, side], axis=1)
     for k in range(blocks + 1):
-        classify(voxels[:, k * LANES : (k + 1) * LANES], palette, classed, k, blocks, group)
+        classify(voxels[:, k * LANES : (k + 1) * LANES], palette, classed, k, blocks)
     for k in range(blocks):
         part = jnp.dot(
             classed[:, k * LANES : (k + 2) * LANES], weights, preferred_element_type=jnp.float32
@@ -98,22 +116,21 @@
         whole = num // (2 * depth)
         frac = (num - whole * (2 * depth)).astype(jnp.float32) / (2.0 * depth.astype(jnp.float32))
         taps.append(
-            lanczos(frac - (lane - CENTER).astype(jnp.float32))
+            lanczos(frac - (lane - CENTER - whole).astype(jnp.float32))
             .astype(jnp.bfloat16)
             .astype(jnp.float32)
         )
 
-    def shift(v, s, column):
-        num = scalars[5 + v, column] * (2 * (depth_rank * slab + s) + 1 - depth)
-        return num // (2 * depth)
-
     base_x = iota((2 * LANES, LANES), 0) - iota((2 * LANES, LANES), 1)
     base_x = jnp.clip(base_x, FAR, LANES - 1 - FAR)
+    for i in range(0, 2 * LANES, 16):
+        for s in range(slab):
+            for v in range(VIEWS):
+                row = taps[0][v * slab + s : v * slab + s + 1]
+                filter_x[s, i : i + 16, v * LANES : (v + 1) * LANES] = lane_pick(
+                    row, base_x[i : i + 16]
+                ).astype(jnp.bfloat16)
     for s in range(slab):
-        for v in range(VIEWS):
-            row = taps[0][v * slab + s : v * slab + s + 1]
-            index = base_x - shift(v, s, 0)
-            filter_x[s, :, v * LANES : (v + 1) * LANES] = lane_pick(row, index).astype(jnp.bfloat16)
 
         def store(v, k, part):
             own[v, s, :, k * LANES : (k + 1) * LANES] = part
@@ -124,22 +141,24 @@
     to = iota((lanes, lanes), 0)
     frm = iota((lanes, lanes), 1)
     even = band_rank % 2 == 0
-    start_a = jnp.where(even, rows, -HALO)
-    start_b = jnp.where(even, -HALO, rows)
-    at = frm % rows
+    start_a = jnp.where(even, rows, -MARGIN)
+    start_b = jnp.where(even, -MARGIN, rows)
     base_y = []
-    for local in (at, jnp.where(at < HALO, at + start_a, at - HALO + start_b)):
+    for each, at in ((rows, frm % rows), (2 * MARGIN, frm % (2 * MARGIN))):
+        local = at
+        if each != rows:
+            local = jnp.where(at < MARGIN, at + start_a, at - MARGIN + start_b)
         world = local + band_rank * rows
-        fits = (to // rows == frm // rows) & (world >= 0) & (world < height)
+        fits = (to // rows == frm // each) & (world >= 0) & (world < height)
         base_y.append(jnp.where(fits, local - to % rows + CENTER, FAR))
-    for v in range(VIEWS):
-        for s in range(slab):
-            row = taps[1][v * slab + s : v * slab + s + 1]
-            for j in range(2):
-                index = base_y[j] - shift(v, s, 1)
-                filter_y[v, s, :, j * lanes : (j + 1) * lanes] = lane_pick(row, index).astype(
-                    jnp.bfloat16
-                )
+    for j in range(2):
+        for i in range(0, lanes, 16):
+            for v in range(VIEWS):
+                for s in range(slab):
+                    row = taps[1][v * slab + s : v * slab + s + 1]
+                    filter_y[v, s, i : i + 16, j * lanes : (j + 1) * lanes] = lane_pick(
+                        row, base_y[j][i : i + 16]
+                    ).astype(jnp.bfloat16)
 
     shape = filter_w.shape
     half = shape[1] // VIEWS
@@ -158,14 +177,18 @@
     slab = own.shape[1]
     lanes, width = own.shape[2:]
     rows = lanes // 4
+    fill = 8 * MARGIN
+    codes_a = got_a[...].astype(jnp.int32)
+    codes_b = got_b[...].astype(jnp.int32)
     for s in range(slab):
+        for v in range(VIEWS):
+            near[v, s, fill:] = jnp.zeros((lanes - fill, width), jnp.bfloat16)
 
         def store(v, k, part):
-            near[v, s, :, k * LANES : (k + 1) * LANES] = part
-
-        voxels = jnp.concatenate(
-            [got_a[s].astype(jnp.int32), got_b[s].astype(jnp.int32)], axis=0
-        )
+            near[v, s, :fill, k * LANES : (k + 1) * LANES] = part
+
+        at = slice(s * MARGIN, (s + 1) * MARGIN)
+        voxels = jnp.concatenate([codes_a[at], codes_b[at]], axis=0)
         shear_columns(voxels, palette[...], filter_x[s], classed, store)
     chunk = 2 * LANES
     for v in range(VIEWS):
@@ -211,7 +234,7 @@
             other = got[v, at].astype(jnp.float32)
             front = jnp.where(mine_front, mine, other)
             back = jnp.where(mine_front, other, mine)
-            alpha = jnp.take_along_axis(front, pick, axis=1, mode="promise_in_bounds")
+            alpha = lane_gather(front, pick)
             merged = front + (1.0 - alpha) * back
             done.append(merged[HALO - MARGIN : HALO - MARGIN + span])
         out[k] = jnp.concatenate(done, axis=0).astype(jnp.bfloat16)
@@ -231,7 +254,7 @@
             part = arrived[at].astype(jnp.float32)[v * span : (v + 1) * span]
             picture = picture + through * part
             through = through * (
-                1.0 - jnp.take_along_axis(part, pick, axis=1, mode="promise_in_bounds")
+                1.0 - lane_gather(part, pick)
             )
         half = filter_w.shape[1] // VIEWS
         final = jnp.dot(
@@ -281,8 +304,8 @@
     )
     voxels = volume.astype(bf16)
     even = lax.axis_index("band") % 2 == 0
-    first = voxels[:, :HALO]
-    last = voxels[:, rows - HALO :]
+    first = voxels[:, :MARGIN].reshape(slab * MARGIN, width)
+    last = voxels[:, rows - MARGIN :].reshape(slab * MARGIN, width)
     send_a = jnp.where(even, last, first)
     send_b = jnp.where(even, first, last)
     got_a = lax.ppermute(send_a, "band", pairs(band_size, 0))
@@ -306,8 +329,8 @@
         slab_kernel,
         (shape(padded, f32), shape(padded, bf16)),
         (
-            pltpu.VMEM((8 * HALO, width + LANES), bf16),
-            pltpu.VMEM((VIEWS, slab, 8 * HALO, width), bf16),
+            pltpu.VMEM((8 * MARGIN, width + LANES), bf16),
+            pltpu.VMEM((VIEWS, slab, lanes, width), bf16),
         ),
         smem,
     )(params, palette, filter_x, filter_y, own, got_a, got_b)

time: 48.5 us -> 47.1 us (0.971)
  waiting for transfers between devices: 2.01 us -> 3.25 us
  Pallas kernels: 11.7 us -> 10.6 us
  blocking collectives: 25.9 us -> 25 us
  starting transfers between devices: 6.34 us -> 5.5 us
    ppermute x1, starting transfers between devices: 4.82 us -> 2.3 us  [body(): got_b = lax.ppermute(send_b, 'band', pairs(band_size, 1))]
    ppermute x1, starting transfers between devices: 1.43 us -> 3.11 us  [body(): got_a = lax.ppermute(send_a, 'band', pairs(band_size, 0))]
    ppermute x1, waiting for transfers between devices: 0.01 us -> 1.33 us  [body(): got_b = lax.ppermute(send_b, 'band', pairs(band_size, 1))]
    pallas_call x4, Pallas kernels: 11.7 us -> 10.6 us  [run(): pl.pallas_call(kernel, out_shape=outs, in_specs=[pl.BlockSpec(memory_spac...]
    all_to_all x1, blocking collectives: 25.9 us -> 25 us  [body(): lax.all_to_all(merged, 'depth', split_axis=0, concat_axis=0, tiled=True,...]
  transfers between devices with their start and end apart: 3 -> 3, of which waited for: 2 -> 2; matrix products, arithmetic and copies ran while one was open for 2% -> 2% of each run, Pallas kernels for 10% -> 9%
where the time goes in v6:
time: 47.1 us; the launch traced here: 46.5 us
  blocking collectives  25 us (53%)
  Pallas kernels  10.6 us (23%)
  starting transfers between devices  5.5 us (12%)
  waiting for transfers between devices  3.25 us (7%)
  other arithmetic  1.97 us (4%)
    all_to_all x1, blocking collectives, body(): lax.all_to_all(merged, 'depth', split_axis=0, concat_axis=0, tiled=True,...  25 us
    pallas_call x4, Pallas kernels, run(): pl.pallas_call(kernel, out_shape=outs, in_specs=[pl.BlockSpec(memory_spac...  10.6 us
    ppermute x1, starting transfers between devices, body(): got_a = lax.ppermute(send_a, 'band', pairs(band_size, 0))  3.11 us
    ppermute x1, starting transfers between devices, body(): got_b = lax.ppermute(send_b, 'band', pairs(band_size, 1))  2.3 us
    ppermute x1, waiting for transfers between devices, body(): got = lax.ppermute(send, 'depth', pairs(depth_size, 0))  1.92 us
    ppermute x1, waiting for transfers between devices, body(): got_b = lax.ppermute(send_b, 'band', pairs(band_size, 1))  1.33 us
    convert_element_type x1, other arithmetic, body(): voxels = volume.astype(bf16)  1.07 us
  transfers between devices with their start and end apart: 3, of which 2 were waited for; matrix products, arithmetic and copies ran while one was open for 2% of the time, Pallas kernels for 9%

profile of v6, /device:TPU:16, one launch (start us, length us, event | category | flops | bytes accessed | tf_op | source)
XLA Modules:
  0.0 46.5 jit_solution(14590824644587619441)
XLA Ops:
  0.0 1.1 %convert_element_type.3.vol = bf16[4,32,1024]{2,1,0:T(8,128)(2,1)S(1)} convert(s32[4,32,1024]{2,1,0:T(8,128)} %param.3) | non-fusion elementwise | flops 131072 | bytes 786432 | tf_op jit(solution)/shard_map/convert_element_type | solution.py:305
  1.2 3.1 %collective-permute-start = (bf16[48,1024]{1,0:T(8,128)(2,1)S(1)}, bf16[48,1024]{1,0:T(8,128)(2,1)S(1)}, u32[]{:S(2)}, u32[]{:S(2)}) collective-permute-start(bf16[48,1024]{1,0:T(8,128)(2,1)S(1)} %select_n.28), channel_id=1, source_target_pairs={{0,1},{1,0},{2,3},{3,2},{4,5},{5,4},{6,7},{7,6},{8,9},{9,8},{10,11... | collective-permute-start | bytes 294920 | tf_op jit(solution)/shard_map/ppermute | solution.py:311
  4.3 2.3 %collective-permute-start.1 = (bf16[48,1024]{1,0:T(8,128)(2,1)S(1)}, bf16[48,1024]{1,0:T(8,128)(2,1)S(1)}, u32[]{:S(2)}, u32[]{:S(2)}) collective-permute-start(bf16[48,1024]{1,0:T(8,128)(2,1)S(1)} %select_n.30), channel_id=1, source_target_pairs={{1,2},{2,1},{3,4},{4,3},{5,6},{6,5},{9,10},{10,9},{11,12},{12,11},... | collective-permute-start | bytes 294920 | tf_op jit(solution)/shard_map/ppermute | solution.py:312
  6.6 0.1 pad.13.clone
  6.7 0.1 add_bitcast_fusion
  6.8 0.8 %fusion.scalars.tables = s32[8,256]{1,0:T(8,128)S(1)} fusion(s32[2,4]{1,0:T(2,128)} %param.5, s32[1,4]{1,0:T(1,128)S(1)} %add_bitcast_fusion, s32[4,256]{1,0:T(4,128)} %param.4, s32[8]{0:T(128)S(1)} %pad.13.clone), kind=kLoop, calls=%fused_computation.3 | loop fusion | flops 6144 | bytes 12368 | tf_op jit(solution)/shard_map/concatenate | solution.py:299
  7.5 4.3 %shard_map.37 = (s32[3,4]{1,0:T(4,128)S(1)}, f32[4,256]{1,0:T(4,128)S(1)}, bf16[2,4,128,1024]{3,2,1,0:T(8,128)(2,1)S(1)}, bf16[4,256,256]{2,1,0:T(8,128)(2,1)S(1...) custom-call(s32[8,256]{1,0:T(8,128)S(1)} %fusion.scalars.tables, s32[8,256]{1,0:T(8,128)S(1)} %fusion.scalars.tables, ...), custom_call_target="tpu_custom_call" | custom-call | tf_op jit(solution)/shard_map/pallas_call | solution.py:274
  11.9 0.0 collective-permute-done.got_a
  11.9 1.3 %collective-permute-done.1.got_b = bf16[48,1024]{1,0:T(8,128)(2,1)S(1)} collective-permute-done((bf16[48,1024]{1,0:T(8,128)(2,1)S(1)}, bf16[48,1024]{1,0:T(8,128)(2,1)S(1)}, u32[]{:S(2)}, u32[]{:S(2)}) %collective-permute-start.1) | collective-permute-done | bytes 98336 | tf_op jit(solution)/shard_map/ppermute | solution.py:312
  13.2 3.4 %shard_map.38 = (f32[2,1056,128]{2,1,0:T(8,128)S(1)}, bf16[2,1056,128]{2,1,0:T(8,128)(2,1)S(1)}) custom-call(s32[3,4]{1,0:T(4,128)S(1)} %get-tuple-element.13.params, f32[4,256]{1,0:T(4,128)S(1)} %get-tuple-element.15.palette, bf16[4,256,256]{2,1,0:T(8,128)(2,1)S(1)} %get-tuple-element.16.filter_x, bf16[2,4,128,256]{3,2,1,0:T(8,128)(2,1)S(1)} %get-tuple-element.17.filter_y, ...), custom_call_target="tpu_custom_call" | custom-call | tf_op jit(solution)/shard_map/pallas_call | solution.py:274
  16.6 0.1 collective-permute-start.2
  16.7 1.9 %collective-permute-done.2.got = bf16[2,1056,128]{2,1,0:T(8,128)(2,1)S(1)} collective-permute-done((bf16[2,1056,128]{2,1,0:T(8,128)(2,1)S(1)}, bf16[2,1056,128]{2,1,0:T(8,128)(2,1)S(1)}, u32[]{:S(2)}, u32[]{:S(2)}) %collective-permute-start.2) | collective-permute-done | bytes 540704 | tf_op jit(solution)/shard_map/ppermute | solution.py:337
  18.6 1.0 %shard_map.39 = bf16[16,112,128]{2,1,0:T(8,128)(2,1)S(1)} custom-call(s32[3,4]{1,0:T(4,128)S(1)} %get-tuple-element.13.params, f32[2,1056,128]{2,1,0:T(8,128)S(1)} %get-tuple-element.19.keep, bf16[2,1056,128]{2,1,0:T(8,128)(2,1)S(1)} %collective-permute-done.2.got), custom_call_target="tpu_custom_call" | custom-call | tf_op jit(solution)/shard_map/pallas_call | solution.py:274
  19.6 25.0 %all_to_all.5.arrived = bf16[16,112,128]{2,1,0:T(8,128)(2,1)S(1)} all-to-all(bf16[16,112,128]{2,1,0:T(8,128)(2,1)S(1)} %shard_map.39), channel_id=1, replica_groups={{0,16,32,48,64,80,96,112,128,144,160,176,192,208,224,240},{8,24,40,56,7..., dimensions={0} | all-to-all | bytes 917504 | tf_op jit(solution)/shard_map/all_to_all | solution.py:340
  44.6 1.9 %shard_map.40 = f32[2,32,4,32]{3,2,1,0:T(4,128)} custom-call(s32[3,4]{1,0:T(4,128)S(1)} %get-tuple-element.13.params, f32[32,128]{1,0:T(8,128)S(1)} %get-tuple-element.14.filter_w, bf16[16,112,128]{2,1,0:T(8,128)(2,1)S(1)} %all_to_all.5.arrived), custom_call_target="tpu_custom_call" | custom-call | tf_op jit(solution)/shard_map/pallas_call | solution.py:274
  (3 shorter events, 0.1 us)
Async XLA Ops:
  1.2 10.7 %collective-permute-start = (bf16[48,1024]{1,0:T(8,128)(2,1)S(1)}, bf16[48,1024]{1,0:T(8,128)(2,1)S(1)}, u32[]{:S(2)}, u32[]{:S(2)}) collective-permute-start(bf16[48,1024]{1,0:T(8,128)(2,1)S(1)} %select_n.28), channel_id=1, source_target_pairs={{0,1},{1,0},{2,3},{3,2},{4,5},{5,4},{6,7},{7,6},{8,9},{9,8},{10,11... | collective-permute-start | bytes 294920 | tf_op jit(solution)/shard_map/ppermute | solution.py:311
  4.3 8.9 %collective-permute-start.1 = (bf16[48,1024]{1,0:T(8,128)(2,1)S(1)}, bf16[48,1024]{1,0:T(8,128)(2,1)S(1)}, u32[]{:S(2)}, u32[]{:S(2)}) collective-permute-start(bf16[48,1024]{1,0:T(8,128)(2,1)S(1)} %select_n.30), channel_id=1, source_target_pairs={{1,2},{2,1},{3,4},{4,3},{5,6},{6,5},{9,10},{10,9},{11,12},{12,11},... | collective-permute-start | bytes 294920 | tf_op jit(solution)/shard_map/ppermute | solution.py:312
  16.6 2.0 %collective-permute-start.2 = (bf16[2,1056,128]{2,1,0:T(8,128)(2,1)S(1)}, bf16[2,1056,128]{2,1,0:T(8,128)(2,1)S(1)}, u32[]{:S(2)}, u32[]{:S(2)}) collective-permute-start(bf16[2,1056,128]{2,1,0:T(8,128)(2,1)S(1)} %get-tuple-element.20), channel_id=1, source_target_pairs={{0,8},{8,0},{16,24},{24,16},{32,40},{40,32},{48,56},{56,48},{64,72... | collective-permute-start | bytes 1622024 | tf_op jit(solution)/shard_map/ppermute | solution.py:337

commit v7 on v6

--- a/solution.py
+++ b/solution.py
@@ -1,3 +1,5 @@
+import functools
+
 import jax
 import jax.numpy as jnp
 from jax import lax
@@ -89,19 +91,14 @@
 
 
 def own_kernel(
-    scalars, tables, vol, params, palette_out, own, filter_x, filter_y, filter_w, classed
+    depth, height, tables, vol, palette_out, own, filter_x, filter_y, filter_w, classed
 ):
     slab, rows, width = vol.shape
-    for i in range(1 + VIEWS):
-        for j in range(4):
-            params[i, j] = scalars[4 + i, j]
-    depth_rank, band_rank = scalars[4, 0], scalars[4, 1]
-    depth = slab * scalars[4, 2]
-    height = rows * scalars[4, 3]
+    depth_rank, band_rank = tables[4:5, 0:1], tables[4:5, 1:2]
     strip = filter_w.shape[0]
 
     codes = tables[0:4].astype(jnp.float32)
-    opacity = codes[3:4] / (64.0 * depth.astype(jnp.float32))
+    opacity = codes[3:4] / (64.0 * depth)
     premult = codes[0:3] / 255.0 * opacity
     palette = jnp.concatenate([premult, opacity], axis=0).astype(jnp.bfloat16).astype(jnp.float32)
     palette_out[...] = palette
@@ -111,10 +108,10 @@
     place = depth_rank * slab + which % slab
     taps = []
     for column in range(2):
-        q = jnp.where(which < slab, scalars[5, column], scalars[6, column])
+        q = jnp.where(which < slab, tables[5:6, column : column + 1], tables[6:7, column : column + 1])
         num = q * (2 * place + 1 - depth)
         whole = num // (2 * depth)
-        frac = (num - whole * (2 * depth)).astype(jnp.float32) / (2.0 * depth.astype(jnp.float32))
+        frac = (num - whole * (2 * depth)).astype(jnp.float32) / (2.0 * depth)
         taps.append(
             lanczos(frac - (lane - CENTER - whole).astype(jnp.float32))
             .astype(jnp.bfloat16)
@@ -164,7 +161,7 @@
     half = shape[1] // VIEWS
     column = iota(shape, 0)
     local = iota(shape, 1) % half - MARGIN
-    q = jnp.where(iota(shape, 1) < half, scalars[5, 2], scalars[6, 2])
+    q = jnp.where(iota(shape, 1) < half, tables[5:6, 2:3], tables[6:7, 2:3])
     num = q * (2 * (depth_rank * strip + column) + 1 - width) + width
     whole = num // (2 * width)
     frac = (num - whole * (2 * width)).astype(jnp.float32) / (2.0 * width)
@@ -172,8 +169,10 @@
 
 
 def slab_kernel(
-    params, palette, filter_x, filter_y, own, got_a, got_b, keep, send, classed, near
+    tables, palette, filter_x, filter_y, own, got_a, got_b, keep, send, classed, near, params, sem
 ):
+    scalars = pltpu.make_async_copy(tables, params, sem)
+    scalars.start()
     slab = own.shape[1]
     lanes, width = own.shape[2:]
     rows = lanes // 4
@@ -190,9 +189,10 @@
         at = slice(s * MARGIN, (s + 1) * MARGIN)
         voxels = jnp.concatenate([codes_a[at], codes_b[at]], axis=0)
         shear_columns(voxels, palette[...], filter_x[s], classed, store)
+    scalars.wait()
     chunk = 2 * LANES
     for v in range(VIEWS):
-        facing = params[1 + v, 3] >= 0
+        facing = params[5 + v, 3] >= 0
         for side in (slice(0, HALO), slice(HALO + width, 2 * HALO + width)):
             keep[v, side] = jnp.zeros((HALO, lanes), jnp.float32)
             send[v, side] = jnp.zeros((HALO, lanes), jnp.bfloat16)
@@ -223,13 +223,13 @@
     span = both // VIEWS
     wide = span + 2 * (HALO - MARGIN)
     rows = lanes // 4
-    core = params[0, 0] % 2
+    core = params[4, 0] % 2
     pick = 3 * rows + iota((wide, lanes), 1) % rows
     for k in range(strips):
         at = pl.ds(pl.multiple_of(k * wide + core * (wide // 2), wide // 2), wide)
         done = []
         for v in range(VIEWS):
-            mine_front = (params[1 + v, 3] >= 0) == (core == 0)
+            mine_front = (params[5 + v, 3] >= 0) == (core == 0)
             mine = keep[v, at]
             other = got[v, at].astype(jnp.float32)
             front = jnp.where(mine_front, mine, other)
@@ -246,7 +246,7 @@
     rows = lanes // 4
     pick = 3 * rows + iota((span, lanes), 1) % rows
     for v in range(VIEWS):
-        facing = params[1 + v, 3] >= 0
+        facing = params[5 + v, 3] >= 0
         picture = jnp.zeros((span, lanes), jnp.float32)
         through = jnp.ones((span, lanes), jnp.float32)
         for k in range(slabs):
@@ -310,10 +310,9 @@
     send_b = jnp.where(even, first, last)
     got_a = lax.ppermute(send_a, "band", pairs(band_size, 0))
     got_b = lax.ppermute(send_b, "band", pairs(band_size, 1))
-    params, palette, own, filter_x, filter_y, filter_w = call(
-        own_kernel,
+    palette, own, filter_x, filter_y, filter_w = call(
+        functools.partial(own_kernel, slab * depth_size, rows * band_size),
         (
-            shape((1 + VIEWS, 4), i32),
             shape(tf_table.shape, f32),
             shape((VIEWS, slab, lanes, width), bf16),
             shape((slab, 2 * LANES, VIEWS * LANES), bf16),
@@ -321,9 +320,7 @@
             shape((strip, VIEWS * (strip + 2 * HALO)), f32),
         ),
         (pltpu.VMEM((lanes, width + LANES), bf16),),
-        smem,
-        (pltpu.SMEM,) + (pltpu.VMEM,) * 5,
-    )(tables, tables, voxels)
+    )(tables, voxels)
     padded = (VIEWS, width + 2 * HALO, lanes)
     keep, send = call(
         slab_kernel,
@@ -331,12 +328,14 @@
         (
             pltpu.VMEM((8 * MARGIN, width + LANES), bf16),
             pltpu.VMEM((VIEWS, slab, lanes, width), bf16),
+            pltpu.SMEM(tables.shape, i32),
+            pltpu.SemaphoreType.DMA(()),
         ),
-        smem,
-    )(params, palette, filter_x, filter_y, own, got_a, got_b)
+        (pl.ANY,),
+    )(tables, palette, filter_x, filter_y, own, got_a, got_b)
     got = lax.ppermute(send, "depth", pairs(depth_size, 0))
     merged = shape((depth_size // 2, VIEWS * (strip + 2 * MARGIN), lanes), bf16)
-    merged = call(merge_kernel, merged, (), smem)(params, keep, got)
+    merged = call(merge_kernel, merged, (), smem)(tables, keep, got)
     arrived = lax.all_to_all(
         merged,
         "depth",
@@ -346,7 +345,7 @@
         axis_index_groups=[list(range(i, depth_size, 2)) for i in range(2)],
     )
     final = shape((VIEWS, strip, 4, rows), f32)
-    return call(final_kernel, final, (), smem)(params, filter_w, arrived)
+    return call(final_kernel, final, (), smem)(tables, filter_w, arrived)
 
 
 def solution(mesh):

time: 47.1 us -> 46.4 us (0.985)
  Pallas kernels: 10.6 us -> 9.34 us
  waiting for transfers between devices: 3.25 us -> 4.23 us
    pallas_call x4, Pallas kernels: 10.6 us -> 9.34 us  [run(): pl.pallas_call(kernel, out_shape=outs, in_specs=[pl.BlockSpec(memory_spac...]
    ppermute x1, waiting for transfers between devices: 1.33 us -> 2.31 us  [body(): got_b = lax.ppermute(send_b, 'band', pairs(band_size, 1))]
  transfers between devices with their start and end apart: 3 -> 3, of which waited for: 2 -> 2; matrix products, arithmetic and copies ran while one was open for 2% -> 2% of each run, Pallas kernels for 9% -> 7%
where the time goes in v7:
time: 46.4 us; the launch traced here: 46.2 us
  blocking collectives  25 us (54%)
  Pallas kernels  9.34 us (20%)
  starting transfers between devices  5.5 us (12%)
  waiting for transfers between devices  4.23 us (9%)
  other arithmetic  1.97 us (4%)
    all_to_all x1, blocking collectives, body(): lax.all_to_all(merged, 'depth', split_axis=0, concat_axis=0, tiled=True,...  25 us
    pallas_call x4, Pallas kernels, run(): pl.pallas_call(kernel, out_shape=outs, in_specs=[pl.BlockSpec(memory_spac...  9.34 us
    ppermute x1, starting transfers between devices, body(): got_a = lax.ppermute(send_a, 'band', pairs(band_size, 0))  3.11 us
    ppermute x1, waiting for transfers between devices, body(): got_b = lax.ppermute(send_b, 'band', pairs(band_size, 1))  2.31 us
    ppermute x1, starting transfers between devices, body(): got_b = lax.ppermute(send_b, 'band', pairs(band_size, 1))  2.3 us
    ppermute x1, waiting for transfers between devices, body(): got = lax.ppermute(send, 'depth', pairs(depth_size, 0))  1.92 us
    convert_element_type x1, other arithmetic, body(): voxels = volume.astype(bf16)  1.07 us
  transfers between devices with their start and end apart: 3, of which 2 were waited for; matrix products, arithmetic and copies ran while one was open for 2% of the time, Pallas kernels for 7%

profile of v7, /device:TPU:16, one launch (start us, length us, event | category | flops | bytes accessed | tf_op | source)
XLA Modules:
  0.0 46.2 jit_solution(17382955946212748790)
XLA Ops:
  0.0 1.1 %convert_element_type.3.vol = bf16[4,32,1024]{2,1,0:T(8,128)(2,1)S(1)} convert(s32[4,32,1024]{2,1,0:T(8,128)} %param.3) | non-fusion elementwise | flops 131072 | bytes 786432 | tf_op jit(solution)/shard_map/convert_element_type | solution.py:305
  1.2 3.1 %collective-permute-start = (bf16[48,1024]{1,0:T(8,128)(2,1)S(1)}, bf16[48,1024]{1,0:T(8,128)(2,1)S(1)}, u32[]{:S(2)}, u32[]{:S(2)}) collective-permute-start(bf16[48,1024]{1,0:T(8,128)(2,1)S(1)} %select_n.28), channel_id=1, source_target_pairs={{0,1},{1,0},{2,3},{3,2},{4,5},{5,4},{6,7},{7,6},{8,9},{9,8},{10,11... | collective-permute-start | bytes 294920 | tf_op jit(solution)/shard_map/ppermute | solution.py:311
  4.3 2.3 %collective-permute-start.1 = (bf16[48,1024]{1,0:T(8,128)(2,1)S(1)}, bf16[48,1024]{1,0:T(8,128)(2,1)S(1)}, u32[]{:S(2)}, u32[]{:S(2)}) collective-permute-start(bf16[48,1024]{1,0:T(8,128)(2,1)S(1)} %select_n.30), channel_id=1, source_target_pairs={{1,2},{2,1},{3,4},{4,3},{5,6},{6,5},{9,10},{10,9},{11,12},{12,11},... | collective-permute-start | bytes 294920 | tf_op jit(solution)/shard_map/ppermute | solution.py:312
  6.6 0.1 pad.13.clone
  6.7 0.1 add_bitcast_fusion
  6.8 0.8 %fusion.tables.params = s32[8,256]{1,0:T(8,128)S(1)} fusion(s32[2,4]{1,0:T(2,128)} %param.5, s32[1,4]{1,0:T(1,128)S(1)} %add_bitcast_fusion, s32[4,256]{1,0:T(4,128)} %param.4, s32[8]{0:T(128)S(1)} %pad.13.clone), kind=kLoop, calls=%fused_computation.3 | loop fusion | flops 6144 | bytes 12368 | tf_op jit(solution)/shard_map/concatenate | solution.py:299
  7.5 3.3 %shard_map.37 = (f32[4,256]{1,0:T(4,128)S(1)}, bf16[2,4,128,1024]{3,2,1,0:T(8,128)(2,1)S(1)}, bf16[4,256,256]{2,1,0:T(8,128)(2,1)S(1)}, bf16[2,4,128,256]{3,2,1,0:T(8,128)(2,1)S(1)}, f32[32,128]{1,0:T(8,128)S(1)}) custom-call(s32[8,256]{1,0:T(8,128)S(1)} %fusion.tables.params, bf16[4,32,1024]{2,1,0:T(8,128)(2,1)S(1)} %convert_element_type.3.vol), custom_call_target="tpu_custom_call" | custom-call | tf_op jit(solution)/shard_map/pallas_call | solution.py:274
  10.9 0.0 collective-permute-done.got_a
  10.9 2.3 %collective-permute-done.1.got_b = bf16[48,1024]{1,0:T(8,128)(2,1)S(1)} collective-permute-done((bf16[48,1024]{1,0:T(8,128)(2,1)S(1)}, bf16[48,1024]{1,0:T(8,128)(2,1)S(1)}, u32[]{:S(2)}, u32[]{:S(2)}) %collective-permute-start.1) | collective-permute-done | bytes 98336 | tf_op jit(solution)/shard_map/ppermute | solution.py:312
  13.2 2.9 %shard_map.38 = (f32[2,1056,128]{2,1,0:T(8,128)S(1)}, bf16[2,1056,128]{2,1,0:T(8,128)(2,1)S(1)}) custom-call(s32[8,256]{1,0:T(8,128)S(1)} %fusion.tables.params, f32[4,256]{1,0:T(4,128)S(1)} %get-tuple-element.13.palette, bf16[4,256,256]{2,1,0:T(8,128)(2,1)S(1)} %get-tuple-element.14.filter_x, bf16[2,4,128,256]{3,2,1,0:T(8,128)(2,1)S(1)} %get-tuple-element.15.filter_y, ...), custom_call_target="tpu_custom_call" | custom-call | tf_op jit(solution)/shard_map/pallas_call | solution.py:274
  16.1 0.1 collective-permute-start.2
  16.2 1.9 %collective-permute-done.2.got = bf16[2,1056,128]{2,1,0:T(8,128)(2,1)S(1)} collective-permute-done((bf16[2,1056,128]{2,1,0:T(8,128)(2,1)S(1)}, bf16[2,1056,128]{2,1,0:T(8,128)(2,1)S(1)}, u32[]{:S(2)}, u32[]{:S(2)}) %collective-permute-start.2) | collective-permute-done | bytes 540704 | tf_op jit(solution)/shard_map/ppermute | solution.py:336
  18.1 1.1 %shard_map.39 = bf16[16,112,128]{2,1,0:T(8,128)(2,1)S(1)} custom-call(s32[8,256]{1,0:T(8,128)S(1)} %fusion.tables.params, f32[2,1056,128]{2,1,0:T(8,128)S(1)} %get-tuple-element.17.keep, bf16[2,1056,128]{2,1,0:T(8,128)(2,1)S(1)} %collective-permute-done.2.got), custom_call_target="tpu_custom_call" | custom-call | tf_op jit(solution)/shard_map/pallas_call | solution.py:274
  19.2 25.0 %all_to_all.5.arrived = bf16[16,112,128]{2,1,0:T(8,128)(2,1)S(1)} all-to-all(bf16[16,112,128]{2,1,0:T(8,128)(2,1)S(1)} %shard_map.39), channel_id=1, replica_groups={{0,16,32,48,64,80,96,112,128,144,160,176,192,208,224,240},{8,24,40,56,7..., dimensions={0} | all-to-all | bytes 917504 | tf_op jit(solution)/shard_map/all_to_all | solution.py:339
  44.2 2.0 %shard_map.40 = f32[2,32,4,32]{3,2,1,0:T(4,128)} custom-call(s32[8,256]{1,0:T(8,128)S(1)} %fusion.tables.params, f32[32,128]{1,0:T(8,128)S(1)} %get-tuple-element.12.filter_w, bf16[16,112,128]{2,1,0:T(8,128)(2,1)S(1)} %all_to_all.5.arrived), custom_call_target="tpu_custom_call" | custom-call | tf_op jit(solution)/shard_map/pallas_call | solution.py:274
  (3 shorter events, 0.1 us)
Async XLA Ops:
  1.2 9.7 %collective-permute-start = (bf16[48,1024]{1,0:T(8,128)(2,1)S(1)}, bf16[48,1024]{1,0:T(8,128)(2,1)S(1)}, u32[]{:S(2)}, u32[]{:S(2)}) collective-permute-start(bf16[48,1024]{1,0:T(8,128)(2,1)S(1)} %select_n.28), channel_id=1, source_target_pairs={{0,1},{1,0},{2,3},{3,2},{4,5},{5,4},{6,7},{7,6},{8,9},{9,8},{10,11... | collective-permute-start | bytes 294920 | tf_op jit(solution)/shard_map/ppermute | solution.py:311
  4.3 8.9 %collective-permute-start.1 = (bf16[48,1024]{1,0:T(8,128)(2,1)S(1)}, bf16[48,1024]{1,0:T(8,128)(2,1)S(1)}, u32[]{:S(2)}, u32[]{:S(2)}) collective-permute-start(bf16[48,1024]{1,0:T(8,128)(2,1)S(1)} %select_n.30), channel_id=1, source_target_pairs={{1,2},{2,1},{3,4},{4,3},{5,6},{6,5},{9,10},{10,9},{11,12},{12,11},... | collective-permute-start | bytes 294920 | tf_op jit(solution)/shard_map/ppermute | solution.py:312
  16.1 2.0 %collective-permute-start.2 = (bf16[2,1056,128]{2,1,0:T(8,128)(2,1)S(1)}, bf16[2,1056,128]{2,1,0:T(8,128)(2,1)S(1)}, u32[]{:S(2)}, u32[]{:S(2)}) collective-permute-start(bf16[2,1056,128]{2,1,0:T(8,128)(2,1)S(1)} %get-tuple-element.18), channel_id=1, source_target_pairs={{0,8},{8,0},{16,24},{24,16},{32,40},{40,32},{48,56},{56,48},{64,72... | collective-permute-start | bytes 1622024 | tf_op jit(solution)/shard_map/ppermute | solution.py:336

commit v8 on v7

--- a/solution.py
+++ b/solution.py
@@ -218,24 +218,30 @@
             send[v, at] = turned.astype(jnp.bfloat16)
 
 
-def merge_kernel(params, keep, got, out):
+def merge_kernel(tables, keep, got, out):
     strips, both, lanes = out.shape
     span = both // VIEWS
     wide = span + 2 * (HALO - MARGIN)
     rows = lanes // 4
-    core = params[4, 0] % 2
-    pick = 3 * rows + iota((wide, lanes), 1) % rows
+    shape = (wide, lanes)
+    core = jnp.broadcast_to(tables[4:5, 0:1] % 2, shape)
+    second = core == 1
+    pick = 3 * rows + iota(shape, 1) % rows
+    forward = [
+        jnp.broadcast_to((tables[5 + v : 6 + v, 3:4] >= 0).astype(jnp.int32), shape)
+        for v in range(VIEWS)
+    ]
     for k in range(strips):
-        at = pl.ds(pl.multiple_of(k * wide + core * (wide // 2), wide // 2), wide)
+        low = slice(k * wide, (k + 1) * wide)
+        high = slice(k * wide + wide // 2, (k + 1) * wide + wide // 2)
         done = []
         for v in range(VIEWS):
-            mine_front = (params[5 + v, 3] >= 0) == (core == 0)
-            mine = keep[v, at]
-            other = got[v, at].astype(jnp.float32)
+            mine_front = forward[v] + core == 1
+            mine = jnp.where(second, keep[v, high], keep[v, low])
+            other = jnp.where(second, got[v, high], got[v, low]).astype(jnp.float32)
             front = jnp.where(mine_front, mine, other)
             back = jnp.where(mine_front, other, mine)
-            alpha = lane_gather(front, pick)
-            merged = front + (1.0 - alpha) * back
+            merged = front + (1.0 - lane_gather(front, pick)) * back
             done.append(merged[HALO - MARGIN : HALO - MARGIN + span])
         out[k] = jnp.concatenate(done, axis=0).astype(jnp.bfloat16)
 
@@ -335,7 +341,7 @@
     )(tables, palette, filter_x, filter_y, own, got_a, got_b)
     got = lax.ppermute(send, "depth", pairs(depth_size, 0))
     merged = shape((depth_size // 2, VIEWS * (strip + 2 * MARGIN), lanes), bf16)
-    merged = call(merge_kernel, merged, (), smem)(tables, keep, got)
+    merged = call(merge_kernel, merged)(tables, keep, got)
     arrived = lax.all_to_all(
         merged,
         "depth",

time: 46.4 us -> 46 us (level)
  Pallas kernels: 9.34 us -> 8.86 us
    pallas_call x4, Pallas kernels: 9.34 us -> 8.86 us  [run(): pl.pallas_call(kernel, out_shape=outs, in_specs=[pl.BlockSpec(memory_spac...]
where the time goes in v8:
time: 46 us; the launch traced here: 45.8 us
  blocking collectives  25 us (54%)
  Pallas kernels  8.86 us (19%)
  starting transfers between devices  5.5 us (12%)
  waiting for transfers between devices  4.23 us (9%)
  other arithmetic  1.97 us (4%)
    all_to_all x1, blocking collectives, body(): lax.all_to_all(merged, 'depth', split_axis=0, concat_axis=0, tiled=True,...  25 us
    pallas_call x4, Pallas kernels, run(): pl.pallas_call(kernel, out_shape=outs, in_specs=[pl.BlockSpec(memory_spac...  8.86 us
    ppermute x1, starting transfers between devices, body(): got_a = lax.ppermute(send_a, 'band', pairs(band_size, 0))  3.11 us
    ppermute x1, waiting for transfers between devices, body(): got_b = lax.ppermute(send_b, 'band', pairs(band_size, 1))  2.31 us
    ppermute x1, starting transfers between devices, body(): got_b = lax.ppermute(send_b, 'band', pairs(band_size, 1))  2.3 us
    ppermute x1, waiting for transfers between devices, body(): got = lax.ppermute(send, 'depth', pairs(depth_size, 0))  1.92 us
    convert_element_type x1, other arithmetic, body(): voxels = volume.astype(bf16)  1.07 us
  transfers between devices with their start and end apart: 3, of which 2 were waited for; matrix products, arithmetic and copies ran while one was open for 2% of the time, Pallas kernels for 7%

profile of v8, /device:TPU:16, one launch (start us, length us, event | category | flops | bytes accessed | tf_op | source)
XLA Modules:
  0.0 45.8 jit_solution(17176123318927591228)
XLA Ops:
  0.0 1.1 %convert_element_type.3.vol = bf16[4,32,1024]{2,1,0:T(8,128)(2,1)S(1)} convert(s32[4,32,1024]{2,1,0:T(8,128)} %param.3) | non-fusion elementwise | flops 131072 | bytes 786432 | tf_op jit(solution)/shard_map/convert_element_type | solution.py:311
  1.2 3.1 %collective-permute-start = (bf16[48,1024]{1,0:T(8,128)(2,1)S(1)}, bf16[48,1024]{1,0:T(8,128)(2,1)S(1)}, u32[]{:S(2)}, u32[]{:S(2)}) collective-permute-start(bf16[48,1024]{1,0:T(8,128)(2,1)S(1)} %select_n.28), channel_id=1, source_target_pairs={{0,1},{1,0},{2,3},{3,2},{4,5},{5,4},{6,7},{7,6},{8,9},{9,8},{10,11... | collective-permute-start | bytes 294920 | tf_op jit(solution)/shard_map/ppermute | solution.py:317
  4.3 2.3 %collective-permute-start.1 = (bf16[48,1024]{1,0:T(8,128)(2,1)S(1)}, bf16[48,1024]{1,0:T(8,128)(2,1)S(1)}, u32[]{:S(2)}, u32[]{:S(2)}) collective-permute-start(bf16[48,1024]{1,0:T(8,128)(2,1)S(1)} %select_n.30), channel_id=1, source_target_pairs={{1,2},{2,1},{3,4},{4,3},{5,6},{6,5},{9,10},{10,9},{11,12},{12,11},... | collective-permute-start | bytes 294920 | tf_op jit(solution)/shard_map/ppermute | solution.py:318
  6.6 0.1 pad.13.clone
  6.7 0.1 add_bitcast_fusion
  6.8 0.8 %fusion.tables.params = s32[8,256]{1,0:T(8,128)S(1)} fusion(s32[2,4]{1,0:T(2,128)} %param.5, s32[1,4]{1,0:T(1,128)S(1)} %add_bitcast_fusion, s32[4,256]{1,0:T(4,128)} %param.4, s32[8]{0:T(128)S(1)} %pad.13.clone), kind=kLoop, calls=%fused_computation.3 | loop fusion | flops 6144 | bytes 12368 | tf_op jit(solution)/shard_map/concatenate | solution.py:305
  7.5 3.3 %shard_map.37 = (f32[4,256]{1,0:T(4,128)S(1)}, bf16[2,4,128,1024]{3,2,1,0:T(8,128)(2,1)S(1)}, bf16[4,256,256]{2,1,0:T(8,128)(2,1)S(1)}, bf16[2,4,128,256]{3,2,1,0:T(8,128)(2,1)S(1)}, f32[32,128]{1,0:T(8,128)S(1)}) custom-call(s32[8,256]{1,0:T(8,128)S(1)} %fusion.tables.params, bf16[4,32,1024]{2,1,0:T(8,128)(2,1)S(1)} %convert_element_type.3.vol), custom_call_target="tpu_custom_call" | custom-call | tf_op jit(solution)/shard_map/pallas_call | solution.py:280
  10.9 0.0 collective-permute-done.got_a
  10.9 2.3 %collective-permute-done.1.got_b = bf16[48,1024]{1,0:T(8,128)(2,1)S(1)} collective-permute-done((bf16[48,1024]{1,0:T(8,128)(2,1)S(1)}, bf16[48,1024]{1,0:T(8,128)(2,1)S(1)}, u32[]{:S(2)}, u32[]{:S(2)}) %collective-permute-start.1) | collective-permute-done | bytes 98336 | tf_op jit(solution)/shard_map/ppermute | solution.py:318
  13.2 2.9 %shard_map.38 = (f32[2,1056,128]{2,1,0:T(8,128)S(1)}, bf16[2,1056,128]{2,1,0:T(8,128)(2,1)S(1)}) custom-call(s32[8,256]{1,0:T(8,128)S(1)} %fusion.tables.params, f32[4,256]{1,0:T(4,128)S(1)} %get-tuple-element.13.palette, bf16[4,256,256]{2,1,0:T(8,128)(2,1)S(1)} %get-tuple-element.14.filter_x, bf16[2,4,128,256]{3,2,1,0:T(8,128)(2,1)S(1)} %get-tuple-element.15.filter_y, ...), custom_call_target="tpu_custom_call" | custom-call | tf_op jit(solution)/shard_map/pallas_call | solution.py:280
  16.1 0.1 collective-permute-start.2
  16.2 1.9 %collective-permute-done.2.got = bf16[2,1056,128]{2,1,0:T(8,128)(2,1)S(1)} collective-permute-done((bf16[2,1056,128]{2,1,0:T(8,128)(2,1)S(1)}, bf16[2,1056,128]{2,1,0:T(8,128)(2,1)S(1)}, u32[]{:S(2)}, u32[]{:S(2)}) %collective-permute-start.2) | collective-permute-done | bytes 540704 | tf_op jit(solution)/shard_map/ppermute | solution.py:342
  18.1 0.6 %shard_map.39 = bf16[16,112,128]{2,1,0:T(8,128)(2,1)S(1)} custom-call(s32[8,256]{1,0:T(8,128)S(1)} %fusion.tables.params, f32[2,1056,128]{2,1,0:T(8,128)S(1)} %get-tuple-element.17.keep, bf16[2,1056,128]{2,1,0:T(8,128)(2,1)S(1)} %collective-permute-done.2.got), custom_call_target="tpu_custom_call" | custom-call | tf_op jit(solution)/shard_map/pallas_call | solution.py:280
  18.8 25.0 %all_to_all.5.arrived = bf16[16,112,128]{2,1,0:T(8,128)(2,1)S(1)} all-to-all(bf16[16,112,128]{2,1,0:T(8,128)(2,1)S(1)} %shard_map.39), channel_id=1, replica_groups={{0,16,32,48,64,80,96,112,128,144,160,176,192,208,224,240},{8,24,40,56,7..., dimensions={0} | all-to-all | bytes 917504 | tf_op jit(solution)/shard_map/all_to_all | solution.py:345
  43.7 2.0 %shard_map.40 = f32[2,32,4,32]{3,2,1,0:T(4,128)} custom-call(s32[8,256]{1,0:T(8,128)S(1)} %fusion.tables.params, f32[32,128]{1,0:T(8,128)S(1)} %get-tuple-element.12.filter_w, bf16[16,112,128]{2,1,0:T(8,128)(2,1)S(1)} %all_to_all.5.arrived), custom_call_target="tpu_custom_call" | custom-call | tf_op jit(solution)/shard_map/pallas_call | solution.py:280
  (3 shorter events, 0.1 us)
Async XLA Ops:
  1.2 9.7 %collective-permute-start = (bf16[48,1024]{1,0:T(8,128)(2,1)S(1)}, bf16[48,1024]{1,0:T(8,128)(2,1)S(1)}, u32[]{:S(2)}, u32[]{:S(2)}) collective-permute-start(bf16[48,1024]{1,0:T(8,128)(2,1)S(1)} %select_n.28), channel_id=1, source_target_pairs={{0,1},{1,0},{2,3},{3,2},{4,5},{5,4},{6,7},{7,6},{8,9},{9,8},{10,11... | collective-permute-start | bytes 294920 | tf_op jit(solution)/shard_map/ppermute | solution.py:317
  4.3 8.9 %collective-permute-start.1 = (bf16[48,1024]{1,0:T(8,128)(2,1)S(1)}, bf16[48,1024]{1,0:T(8,128)(2,1)S(1)}, u32[]{:S(2)}, u32[]{:S(2)}) collective-permute-start(bf16[48,1024]{1,0:T(8,128)(2,1)S(1)} %select_n.30), channel_id=1, source_target_pairs={{1,2},{2,1},{3,4},{4,3},{5,6},{6,5},{9,10},{10,9},{11,12},{12,11},... | collective-permute-start | bytes 294920 | tf_op jit(solution)/shard_map/ppermute | solution.py:318
  16.1 2.0 %collective-permute-start.2 = (bf16[2,1056,128]{2,1,0:T(8,128)(2,1)S(1)}, bf16[2,1056,128]{2,1,0:T(8,128)(2,1)S(1)}, u32[]{:S(2)}, u32[]{:S(2)}) collective-permute-start(bf16[2,1056,128]{2,1,0:T(8,128)(2,1)S(1)} %get-tuple-element.18), channel_id=1, source_target_pairs={{0,8},{8,0},{16,24},{24,16},{32,40},{40,32},{48,56},{56,48},{64,72... | collective-permute-start | bytes 1622024 | tf_op jit(solution)/shard_map/ppermute | solution.py:342

commit v9 on v8

--- a/solution.py
+++ b/solution.py
@@ -246,18 +246,19 @@
         out[k] = jnp.concatenate(done, axis=0).astype(jnp.bfloat16)
 
 
-def final_kernel(params, filter_w, arrived, out):
+def final_kernel(tables, filter_w, arrived, out):
     slabs, both, lanes = arrived.shape
     span = both // VIEWS
     rows = lanes // 4
     pick = 3 * rows + iota((span, lanes), 1) % rows
     for v in range(VIEWS):
-        facing = params[5 + v, 3] >= 0
+        facing = jnp.broadcast_to(tables[5 + v : 6 + v, 3:4], (both, lanes)) >= 0
         picture = jnp.zeros((span, lanes), jnp.float32)
         through = jnp.ones((span, lanes), jnp.float32)
         for k in range(slabs):
-            at = jnp.where(facing, k, slabs - 1 - k)
-            part = arrived[at].astype(jnp.float32)[v * span : (v + 1) * span]
+            ahead = arrived[k].astype(jnp.float32)
+            behind = arrived[slabs - 1 - k].astype(jnp.float32)
+            part = jnp.where(facing, ahead, behind)[v * span : (v + 1) * span]
             picture = picture + through * part
             through = through * (
                 1.0 - lane_gather(part, pick)
@@ -351,7 +352,7 @@
         axis_index_groups=[list(range(i, depth_size, 2)) for i in range(2)],
     )
     final = shape((VIEWS, strip, 4, rows), f32)
-    return call(final_kernel, final, (), smem)(tables, filter_w, arrived)
+    return call(final_kernel, final)(tables, filter_w, arrived)
 
 
 def solution(mesh):

time: 46 us -> 45.4 us (0.987)
  Pallas kernels: 8.86 us -> 8.25 us
    pallas_call x4, Pallas kernels: 8.86 us -> 8.25 us  [run(): pl.pallas_call(kernel, out_shape=outs, in_specs=[pl.BlockSpec(memory_spac...]
where the time goes in v9:
time: 45.4 us; the launch traced here: 45.2 us
  blocking collectives  25 us (55%)
  Pallas kernels  8.25 us (18%)
  starting transfers between devices  5.5 us (12%)
  waiting for transfers between devices  4.23 us (9%)
  other arithmetic  1.97 us (4%)
    all_to_all x1, blocking collectives, body(): lax.all_to_all(merged, 'depth', split_axis=0, concat_axis=0, tiled=True,...  25 us
    pallas_call x4, Pallas kernels, run(): pl.pallas_call(kernel, out_shape=outs, in_specs=[pl.BlockSpec(memory_spac...  8.25 us
    ppermute x1, starting transfers between devices, body(): got_a = lax.ppermute(send_a, 'band', pairs(band_size, 0))  3.11 us
    ppermute x1, waiting for transfers between devices, body(): got_b = lax.ppermute(send_b, 'band', pairs(band_size, 1))  2.31 us
    ppermute x1, starting transfers between devices, body(): got_b = lax.ppermute(send_b, 'band', pairs(band_size, 1))  2.3 us
    ppermute x1, waiting for transfers between devices, body(): got = lax.ppermute(send, 'depth', pairs(depth_size, 0))  1.92 us
    convert_element_type x1, other arithmetic, body(): voxels = volume.astype(bf16)  1.07 us
  transfers between devices with their start and end apart: 3, of which 2 were waited for; matrix products, arithmetic and copies ran while one was open for 2% of the time, Pallas kernels for 7%

profile of v9, /device:TPU:16, one launch (start us, length us, event | category | flops | bytes accessed | tf_op | source)
XLA Modules:
  0.0 45.2 jit_solution(12319601227339851697)
XLA Ops:
  0.0 1.1 %convert_element_type.3.vol = bf16[4,32,1024]{2,1,0:T(8,128)(2,1)S(1)} convert(s32[4,32,1024]{2,1,0:T(8,128)} %param.3) | non-fusion elementwise | flops 131072 | bytes 786432 | tf_op jit(solution)/shard_map/convert_element_type | solution.py:312
  1.2 3.1 %collective-permute-start = (bf16[48,1024]{1,0:T(8,128)(2,1)S(1)}, bf16[48,1024]{1,0:T(8,128)(2,1)S(1)}, u32[]{:S(2)}, u32[]{:S(2)}) collective-permute-start(bf16[48,1024]{1,0:T(8,128)(2,1)S(1)} %select_n.28), channel_id=1, source_target_pairs={{0,1},{1,0},{2,3},{3,2},{4,5},{5,4},{6,7},{7,6},{8,9},{9,8},{10,11... | collective-permute-start | bytes 294920 | tf_op jit(solution)/shard_map/ppermute | solution.py:318
  4.3 2.3 %collective-permute-start.1 = (bf16[48,1024]{1,0:T(8,128)(2,1)S(1)}, bf16[48,1024]{1,0:T(8,128)(2,1)S(1)}, u32[]{:S(2)}, u32[]{:S(2)}) collective-permute-start(bf16[48,1024]{1,0:T(8,128)(2,1)S(1)} %select_n.30), channel_id=1, source_target_pairs={{1,2},{2,1},{3,4},{4,3},{5,6},{6,5},{9,10},{10,9},{11,12},{12,11},... | collective-permute-start | bytes 294920 | tf_op jit(solution)/shard_map/ppermute | solution.py:319
  6.6 0.1 pad.13.clone
  6.7 0.1 add_bitcast_fusion
  6.8 0.8 %fusion.tables = s32[8,256]{1,0:T(8,128)S(1)} fusion(s32[2,4]{1,0:T(2,128)} %param.5, s32[1,4]{1,0:T(1,128)S(1)} %add_bitcast_fusion, s32[4,256]{1,0:T(4,128)} %param.4, s32[8]{0:T(128)S(1)} %pad.13.clone), kind=kLoop, calls=%fused_computation.3 | loop fusion | flops 6144 | bytes 12368 | tf_op jit(solution)/shard_map/concatenate | solution.py:306
  7.5 3.3 %shard_map.37 = (f32[4,256]{1,0:T(4,128)S(1)}, bf16[2,4,128,1024]{3,2,1,0:T(8,128)(2,1)S(1)}, bf16[4,256,256]{2,1,0:T(8,128)(2,1)S(1)}, bf16[2,4,128,256]{3,2,1,0:T(8,128)(2,1)S(1)}, f32[32,128]{1,0:T(8,128)S(1)}) custom-call(s32[8,256]{1,0:T(8,128)S(1)} %fusion.tables, bf16[4,32,1024]{2,1,0:T(8,128)(2,1)S(1)} %convert_element_type.3.vol), custom_call_target="tpu_custom_call" | custom-call | tf_op jit(solution)/shard_map/pallas_call | solution.py:281
  10.9 0.0 collective-permute-done.got_a
  10.9 2.3 %collective-permute-done.1.got_b = bf16[48,1024]{1,0:T(8,128)(2,1)S(1)} collective-permute-done((bf16[48,1024]{1,0:T(8,128)(2,1)S(1)}, bf16[48,1024]{1,0:T(8,128)(2,1)S(1)}, u32[]{:S(2)}, u32[]{:S(2)}) %collective-permute-start.1) | collective-permute-done | bytes 98336 | tf_op jit(solution)/shard_map/ppermute | solution.py:319
  13.2 2.9 %shard_map.38 = (f32[2,1056,128]{2,1,0:T(8,128)S(1)}, bf16[2,1056,128]{2,1,0:T(8,128)(2,1)S(1)}) custom-call(s32[8,256]{1,0:T(8,128)S(1)} %fusion.tables, f32[4,256]{1,0:T(4,128)S(1)} %get-tuple-element.13.palette, bf16[4,256,256]{2,1,0:T(8,128)(2,1)S(1)} %get-tuple-element.14.filter_x, bf16[2,4,128,256]{3,2,1,0:T(8,128)(2,1)S(1)} %get-tuple-element.15.filter_y, ...), custom_call_target="tpu_custom_call" | custom-call | tf_op jit(solution)/shard_map/pallas_call | solution.py:281
  16.1 0.1 collective-permute-start.2
  16.2 1.9 %collective-permute-done.2.got = bf16[2,1056,128]{2,1,0:T(8,128)(2,1)S(1)} collective-permute-done((bf16[2,1056,128]{2,1,0:T(8,128)(2,1)S(1)}, bf16[2,1056,128]{2,1,0:T(8,128)(2,1)S(1)}, u32[]{:S(2)}, u32[]{:S(2)}) %collective-permute-start.2) | collective-permute-done | bytes 540704 | tf_op jit(solution)/shard_map/ppermute | solution.py:343
  18.1 0.6 %shard_map.39 = bf16[16,112,128]{2,1,0:T(8,128)(2,1)S(1)} custom-call(s32[8,256]{1,0:T(8,128)S(1)} %fusion.tables, f32[2,1056,128]{2,1,0:T(8,128)S(1)} %get-tuple-element.17.keep, bf16[2,1056,128]{2,1,0:T(8,128)(2,1)S(1)} %collective-permute-done.2.got), custom_call_target="tpu_custom_call" | custom-call | tf_op jit(solution)/shard_map/pallas_call | solution.py:281
  18.8 25.0 %all_to_all.5.arrived = bf16[16,112,128]{2,1,0:T(8,128)(2,1)S(1)} all-to-all(bf16[16,112,128]{2,1,0:T(8,128)(2,1)S(1)} %shard_map.39), channel_id=1, replica_groups={{0,16,32,48,64,80,96,112,128,144,160,176,192,208,224,240},{8,24,40,56,7..., dimensions={0} | all-to-all | bytes 917504 | tf_op jit(solution)/shard_map/all_to_all | solution.py:346
  43.7 1.4 %shard_map.40 = f32[2,32,4,32]{3,2,1,0:T(4,128)} custom-call(s32[8,256]{1,0:T(8,128)S(1)} %fusion.tables, f32[32,128]{1,0:T(8,128)S(1)} %get-tuple-element.12.filter_w, bf16[16,112,128]{2,1,0:T(8,128)(2,1)S(1)} %all_to_all.5.arrived), custom_call_target="tpu_custom_call" | custom-call | tf_op jit(solution)/shard_map/pallas_call | solution.py:281
  (3 shorter events, 0.1 us)
Async XLA Ops:
  1.2 9.7 %collective-permute-start = (bf16[48,1024]{1,0:T(8,128)(2,1)S(1)}, bf16[48,1024]{1,0:T(8,128)(2,1)S(1)}, u32[]{:S(2)}, u32[]{:S(2)}) collective-permute-start(bf16[48,1024]{1,0:T(8,128)(2,1)S(1)} %select_n.28), channel_id=1, source_target_pairs={{0,1},{1,0},{2,3},{3,2},{4,5},{5,4},{6,7},{7,6},{8,9},{9,8},{10,11... | collective-permute-start | bytes 294920 | tf_op jit(solution)/shard_map/ppermute | solution.py:318
  4.3 8.9 %collective-permute-start.1 = (bf16[48,1024]{1,0:T(8,128)(2,1)S(1)}, bf16[48,1024]{1,0:T(8,128)(2,1)S(1)}, u32[]{:S(2)}, u32[]{:S(2)}) collective-permute-start(bf16[48,1024]{1,0:T(8,128)(2,1)S(1)} %select_n.30), channel_id=1, source_target_pairs={{1,2},{2,1},{3,4},{4,3},{5,6},{6,5},{9,10},{10,9},{11,12},{12,11},... | collective-permute-start | bytes 294920 | tf_op jit(solution)/shard_map/ppermute | solution.py:319
  16.1 2.0 %collective-permute-start.2 = (bf16[2,1056,128]{2,1,0:T(8,128)(2,1)S(1)}, bf16[2,1056,128]{2,1,0:T(8,128)(2,1)S(1)}, u32[]{:S(2)}, u32[]{:S(2)}) collective-permute-start(bf16[2,1056,128]{2,1,0:T(8,128)(2,1)S(1)} %get-tuple-element.18), channel_id=1, source_target_pairs={{0,8},{8,0},{16,24},{24,16},{32,40},{40,32},{48,56},{56,48},{64,72... | collective-permute-start | bytes 1622024 | tf_op jit(solution)/shard_map/ppermute | solution.py:343
